TPU v7x, 256 devices: a whole 4x4x8 slice. The times are simulated.
256 devices in a mesh: row: 8 (over x, z_lo), col: 32 (over z_hi, y, core).
Axes of the slice: x: 4, y: 4, z: 8 (z_hi: 4, z_lo: 2; z = z_hi * 2 + z_lo), core: 2. Of those that a mesh axis runs over, the one named last changes fastest.
Arguments:
- tile_values: float32 [8, 32, 64, 128, 128], P('row', 'col'), may hold values from -0.15625 to 0.15625
- tile_rows: int32 [8, 32, 64], P('row', 'col'), may hold values from 0 to 159, as said below
- tile_cols: int32 [8, 32, 64], P('row', 'col'), may hold values from 0 to 23
- x_start: float32 [768, 128], P('col', 'row'), may hold values from -6 to 6
- z_start: float32 [1280, 128], P('row'), may hold values from -6 to 6
- y_start: float32 [1280, 128], P('row'), may hold values from -3 to 3
- lower_bound: float32 [1280, 128], P('row'), may hold values from -1.5 to -0.1
- upper_bound: float32 [1280, 128], P('row'), may hold values from 0.1 to 1.5
- cost_diag: float32 [768, 128], P('col', 'row'), may hold values from 0.1 to 10
- linear: float32 [768, 128], P('col', 'row'), may hold values from -6 to 6
- penalty: float32 [1], replicated, may hold values from 0.3 to 3
- proximal: float32 [1], replicated, may hold values from 0.1 to 1
- relaxation: float32 [1], replicated, may hold values from 1.2 to 1.8
Outputs:
- x_next: float32 [768, 128], P('col', 'row')
- z_next: float32 [1280, 128], P('row')
- y_next: float32 [1280, 128], P('row')
Inputs may be any that keep to these rules, and one draw needn't show every extreme that they name: On each device the 64 pairs (tile_rows, tile_cols) are distinct.
All inputs are finite; a program needn't handle non-finite values.
Results may differ from a plain program's by a relative error of at most 0.0002.
Values sent between devices are 32-bit elements; how exact they have to be, the bound alone decides.
A program may use at most 64 MiB of HBM per device.

v0:
```python
import jax
import jax.numpy as jnp
from jax import lax
from jax.sharding import PartitionSpec as P

ADMM_ITERS = 2


HIGH = lax.Precision.HIGHEST


def total_of_pieces(array, axis):
    return lax.all_gather(array, axis).sum(0)


def from_everyone(array, axis):
    copies = jnp.broadcast_to(array, (lax.axis_size(axis), *array.shape))
    return lax.all_to_all(copies, axis, split_axis=0, concat_axis=0, tiled=True)


def of_everyone(array, axis):
    everything = from_everyone(array, axis)
    return jnp.sum(everything, axis=0)


def turned_gather(arrays, axis, dims):
    turned = [jnp.moveaxis(a, dim, 0) for a, dim in zip(arrays, dims)]
    widths = [t[0].size for t in turned]
    both = jnp.concatenate([t.reshape(-1, w) for t, w in zip(turned, widths)], axis=1)
    out = lax.all_gather(both, axis, axis=0, tiled=True)
    parts = jnp.split(out, [sum(widths[:k]) for k in range(1, len(widths))], axis=1)
    return tuple(
        (
            jnp.moveaxis(b.reshape(-1, *t.shape[1:]), 0, dim)
            for b, t, dim in zip(parts, turned, dims)
        )
    )


def shards(
    tile_values,
    tile_rows,
    tile_cols,
    x_start,
    z_start,
    y_start,
    lower_bound,
    upper_bound,
    cost_diag,
    linear,
    penalty,
    proximal,
    relaxation,
):
    order_size = tile_values.shape[3]
    flat_tiles = tile_values.reshape(-1, order_size, order_size)
    row_index = tile_rows.reshape(-1)
    col_index = tile_cols.reshape(-1)
    count_tiles = row_index.shape[0]
    block_rows = z_start.shape[0]
    block_cols = x_start.shape[0]
    row_table = (
        lax.broadcasted_iota(jnp.int32, (block_rows, count_tiles), 0) == row_index[None, :]
    ).astype(jnp.float32)
    col_table = (
        lax.broadcasted_iota(jnp.int32, (block_cols, count_tiles), 0) == col_index[None, :]
    ).astype(jnp.float32)
    rho_value = penalty[0]
    sigma_value = proximal[0]
    relax_value = relaxation[0]
    empty_rows = jnp.zeros((block_rows, order_size), jnp.float32)

    def forward_terms(segment):
        piece_width = segment.shape[1]
        picked = jnp.take(segment, col_index, axis=0)
        products = jnp.einsum("kij,kj->ki", flat_tiles, picked, precision=HIGH)
        return jnp.dot(row_table, products, precision=HIGH)

    def apply_forward(vector):
        local_part = forward_terms(vector)
        return total_of_pieces(local_part, "col")

    def apply_backward(weights_rows):
        picked = jnp.take(weights_rows, row_index, axis=0)
        products = jnp.einsum("kij,ki->kj", flat_tiles, picked, precision=HIGH)
        local_part = jnp.dot(col_table, products, precision=HIGH)
        return of_everyone(local_part, "row")

    def global_totals(values):
        stacked = jnp.stack([jnp.sum(value) for value in values])
        return of_everyone(stacked, "col")

    x_now, diag_now, linear_now = turned_gather((x_start, cost_diag, linear), "row", (1, 1, 1))
    z_now, y_now = (z_start, y_start)
    image_now = empty_rows
    for outer_round in range(ADMM_ITERS):
        if outer_round == 0:
            image_now = apply_forward(x_now)
        target = rho_value * z_now - y_now - rho_value * image_now
        residual = -linear_now - diag_now * x_now + apply_backward(target)
        guess = x_now
        direction = residual
        image_sum = image_now
        norm_now = jnp.float32(1.0)
        norm_now = global_totals([residual * residual])[0]
        pushed = apply_forward(direction)
        applied = (diag_now + sigma_value) * direction + rho_value * apply_backward(pushed)
        curvature = global_totals([direction * applied])[0]
        step_length = norm_now / curvature
        guess = guess + step_length * direction
        image_sum = image_sum + step_length * pushed
        residual = residual - step_length * applied
        image_now = relax_value * image_sum + (1.0 - relax_value) * image_now
        x_now = relax_value * guess + (1.0 - relax_value) * x_now
        mixed = relax_value * image_sum + (1.0 - relax_value) * z_now
        z_fresh = jnp.minimum(jnp.maximum(mixed + y_now / rho_value, lower_bound), upper_bound)
        y_now = y_now + rho_value * (mixed - z_fresh)
        z_now = z_fresh
    piece_width = x_start.shape[1]
    x_now = lax.dynamic_slice_in_dim(x_now, lax.axis_index("row") * piece_width, piece_width, 1)
    return (x_now, z_now, y_now)


def solution(mesh):
    placed = (
        P("row", "col", None, None, None),
        P("row", "col", None),
        P("row", "col", None),
        P("col", "row"),
        P("row", None),
        P("row", None),
        P("row", None),
        P("row", None),
        P("col", "row"),
        P("col", "row"),
        P(),
        P(),
        P(),
    )
    return jax.shard_map(
        shards,
        mesh=mesh,
        in_specs=placed,
        out_specs=(P("col", "row"), P("row", None), P("row", None)),
        check_vma=False,
    )
```

profile of v0, /device:TPU:1, one launch (start us, length us, event | category | flops | bytes accessed | tf_op | source)
XLA Modules:
  0.0 375.3 jit_solution(2561918909377386901)
XLA Ops:
  7.2 0.7 compare_select_fusion.1
  7.9 0.7 compare_and_fusion.1
  8.6 0.8 pad_maximum_fusion
  9.4 23.0 %all_gather.21 = f32[128,72]{1,0:T(8,128)S(1)} all-gather(f32[16,72]{1,0:T(8,128)S(1)} %pad_maximum_fusion), channel_id=1, replica_groups=mesh['row'=8,'col'=32] {'row'}, dimensions={0}, use_global_device_ids=true | all-gather | bytes 41472 | tf_op jit(solution)/shard_map/all_gather | solution.py:30
  33.3 8.3 %fusion.12 = f32[64,1,128]{2,1,0:T(1,128)S(1)} fusion(f32[64,128,1]{1,2,0:T(1,128)S(1)} %bitcast.125, f32[1,1,64,128,128]{4,3,2,1,0:T(8,128)} %param.17), kind=kOutput, calls=%fused_computation.19 | convolution fusion | flops 12582912 | bytes 4259840 | tf_op jit(solution)/shard_map/kij,kj->ki/dot_general | solution.py:76
  41.6 0.8 fusion.16
  43.2 63.6 %all-gather.7.cloned.1.call-done = f32[5120,128]{1,0:T(8,128)} async-done(((f32[160,128]{1,0:T(8,128)}), f32[5120,128]{1,0:T(8,128)}) %all-gather.7.cloned.1.call-update) | async-done | bytes 2621456 | tf_op jit(solution)/shard_map/all_gather | solution.py:13
  106.7 1.9 reduce_sum.135
  109.3 5.3 %fusion.10 = f32[64,1,128]{2,1,0:T(1,128)S(1)} fusion(f32[64,128,1]{1,2,0:T(1,128)S(1)} %bitcast.126, f32[1,1,64,128,128]{4,3,2,1,0:T(8,128)} %param.17), kind=kOutput, calls=%fused_computation.17 | convolution fusion | flops 12582912 | bytes 4259840 | tf_op jit(solution)/shard_map/kij,ki->kj/dot_general | solution.py:85
  114.7 0.6 broadcast_in_dim.42
  115.4 4.0 %all-to-all-start = ((f32[8,24,128]{2,1,0:T(8,128)}), f32[8,24,128]{2,1,0:T(8,128)S(1)}, u32[]{:S(2)}, u32[]{:S(2)}) async-start(f32[8,24,128]{2,1,0:T(8,128)} %broadcast_in_dim.42), calls=%async_computation | async-start | bytes 196608 | tf_op jit(solution)/shard_map/all_to_all | solution.py:18
  119.5 5.2 %all-to-all-done = f32[8,24,128]{2,1,0:T(8,128)S(1)} async-done(((f32[8,24,128]{2,1,0:T(8,128)}), f32[8,24,128]{2,1,0:T(8,128)S(1)}, u32[]{:S(2)}, u32[]{:S(2)}) %all-to-all-start) | async-done | bytes 98336 | tf_op jit(solution)/shard_map/all_to_all | solution.py:18
  125.5 8.3 %fusion.8 = f32[64,1,128]{2,1,0:T(1,128)S(1)} fusion(f32[64,128,1]{1,2,0:T(1,128)S(1)} %bitcast.128, f32[1,1,64,128,128]{4,3,2,1,0:T(8,128)} %param.17), kind=kOutput, calls=%fused_computation.15 | convolution fusion | flops 12582912 | bytes 4259840 | tf_op jit(solution)/shard_map/kij,kj->ki/dot_general | solution.py:76
  133.8 0.8 fusion.15
  134.6 52.7 %all-gather.9.cloned.1.call-done = f32[5120,128]{1,0:T(8,128)} async-done(((f32[160,128]{1,0:T(8,128)}), f32[5120,128]{1,0:T(8,128)}) %all-gather.9.cloned.1.call-update) | async-done | bytes 2621456 | tf_op jit(solution)/shard_map/all_gather | solution.py:13
  187.3 1.9 reduce_sum.139
  189.8 5.3 %fusion.6 = f32[64,1,128]{2,1,0:T(1,128)S(1)} fusion(f32[64,128,1]{1,2,0:T(1,128)S(1)} %bitcast.129, f32[1,1,64,128,128]{4,3,2,1,0:T(8,128)} %param.17), kind=kOutput, calls=%fused_computation.13 | convolution fusion | flops 12582912 | bytes 4259840 | tf_op jit(solution)/shard_map/kij,ki->kj/dot_general | solution.py:85
  195.3 0.6 broadcast_in_dim.44
  195.9 4.0 %all-to-all-start.2 = ((f32[8,24,128]{2,1,0:T(8,128)}), f32[8,24,128]{2,1,0:T(8,128)S(1)}, u32[]{:S(2)}, u32[]{:S(2)}) async-start(f32[8,24,128]{2,1,0:T(8,128)} %broadcast_in_dim.44), calls=%async_computation.2 | async-start | bytes 196608 | tf_op jit(solution)/shard_map/all_to_all | solution.py:18
  200.5 4.7 %all-to-all-done.2 = f32[8,24,128]{2,1,0:T(8,128)S(1)} async-done(((f32[8,24,128]{2,1,0:T(8,128)}), f32[8,24,128]{2,1,0:T(8,128)S(1)}, u32[]{:S(2)}, u32[]{:S(2)}) %all-to-all-start.2) | async-done | bytes 98336 | tf_op jit(solution)/shard_map/all_to_all | solution.py:18
  205.9 0.7 broadcast_in_dim.43
  206.6 16.7 %all_to_all.44 = f32[32,1,1]{2,1,0:T(1,128)S(1)} all-to-all(f32[32,1,1]{2,1,0:T(1,128)S(1)} %broadcast_in_dim.43), channel_id=1, replica_groups=mesh['row'=8,'col'=32] {'col'}, dimensions={0} | all-to-all | bytes 256 | tf_op jit(solution)/shard_map/all_to_all | solution.py:18
  223.2 1.3 broadcast_in_dim.45
  224.5 4.1 %all-to-all-start.3 = ((f32[32,1,1]{2,1,0:T(1,128)}), f32[32,1,1]{2,1,0:T(1,128)S(1)}, u32[]{:S(2)}, u32[]{:S(2)}) async-start(f32[32,1,1]{2,1,0:T(1,128)} %broadcast_in_dim.45), calls=%async_computation.3 | async-start | bytes 32768 | tf_op jit(solution)/shard_map/all_to_all | solution.py:18
  229.5 0.6 reduce_sum.138
  230.2 7.9 %all-to-all-done.3 = f32[32,1,1]{2,1,0:T(1,128)S(1)} async-done(((f32[32,1,1]{2,1,0:T(1,128)}), f32[32,1,1]{2,1,0:T(1,128)S(1)}, u32[]{:S(2)}, u32[]{:S(2)}) %all-to-all-start.3) | async-done | bytes 160 | tf_op jit(solution)/shard_map/all_to_all | solution.py:18
  238.1 0.6 reduce_sum.142
  240.8 5.3 %fusion.4 = f32[64,1,128]{2,1,0:T(1,128)S(1)} fusion(f32[64,128,1]{1,2,0:T(1,128)S(1)} %bitcast.131, f32[1,1,64,128,128]{4,3,2,1,0:T(8,128)} %param.17), kind=kOutput, calls=%fused_computation.11 | convolution fusion | flops 12582912 | bytes 4259840 | tf_op jit(solution)/shard_map/kij,ki->kj/dot_general | solution.py:85
  246.3 7.8 %all_to_all.45 = f32[8,24,128]{2,1,0:T(8,128)S(1)} all-to-all(f32[8,24,128]{2,1,0:T(8,128)S(1)} %broadcast_in_dim.46), channel_id=1, replica_groups=mesh['row'=8,'col'=32] {'row'}, dimensions={0} | all-to-all | bytes 196608 | tf_op jit(solution)/shard_map/all_to_all | solution.py:18
  254.8 8.3 %fusion.2 = f32[64,1,128]{2,1,0:T(1,128)S(1)} fusion(f32[64,128,1]{1,2,0:T(1,128)S(1)} %bitcast.123, f32[1,1,64,128,128]{4,3,2,1,0:T(8,128)} %param.17), kind=kOutput, calls=%fused_computation.9 | convolution fusion | flops 12582912 | bytes 4259840 | tf_op jit(solution)/shard_map/kij,kj->ki/dot_general | solution.py:76
  263.1 0.8 fusion.14
  263.9 49.7 %all-gather.11.cloned.1.call-done = f32[5120,128]{1,0:T(8,128)} async-done(((f32[160,128]{1,0:T(8,128)}), f32[5120,128]{1,0:T(8,128)}) %all-gather.11.cloned.1.call-update) | async-done | bytes 2621456 | tf_op jit(solution)/shard_map/all_gather | solution.py:13
  313.7 1.9 reduce_sum.146
  316.2 5.3 %fusion = f32[64,1,128]{2,1,0:T(1,128)S(1)} fusion(f32[64,128,1]{1,2,0:T(1,128)S(1)} %bitcast.124, f32[1,1,64,128,128]{4,3,2,1,0:T(8,128)} %param.17), kind=kOutput, calls=%fused_computation.7 | convolution fusion | flops 12582912 | bytes 4259840 | tf_op jit(solution)/shard_map/kij,ki->kj/dot_general | solution.py:85
  321.6 0.6 broadcast_in_dim.48
  322.3 4.0 %all-to-all-start.6 = ((f32[8,24,128]{2,1,0:T(8,128)}), f32[8,24,128]{2,1,0:T(8,128)S(1)}, u32[]{:S(2)}, u32[]{:S(2)}) async-start(f32[8,24,128]{2,1,0:T(8,128)} %broadcast_in_dim.48), calls=%async_computation.6 | async-start | bytes 196608 | tf_op jit(solution)/shard_map/all_to_all | solution.py:18
  326.3 5.4 %all-to-all-done.6 = f32[8,24,128]{2,1,0:T(8,128)S(1)} async-done(((f32[8,24,128]{2,1,0:T(8,128)}), f32[8,24,128]{2,1,0:T(8,128)S(1)}, u32[]{:S(2)}, u32[]{:S(2)}) %all-to-all-start.6) | async-done | bytes 98336 | tf_op jit(solution)/shard_map/all_to_all | solution.py:18
  331.7 0.7 multiply_reduce_fusion
  332.4 1.3 broadcast_in_dim.47
  333.7 7.5 %all-to-all-start.5 = ((f32[32,1,1]{2,1,0:T(1,128)}), f32[32,1,1]{2,1,0:T(1,128)S(1)}, u32[]{:S(2)}, u32[]{:S(2)}) async-start(f32[32,1,1]{2,1,0:T(1,128)} %broadcast_in_dim.47), calls=%async_computation.5 | async-start | bytes 32768 | tf_op jit(solution)/shard_map/all_to_all | solution.py:18
  341.2 9.3 %all-to-all-done.5 = f32[32,1,1]{2,1,0:T(1,128)S(1)} async-done(((f32[32,1,1]{2,1,0:T(1,128)}), f32[32,1,1]{2,1,0:T(1,128)S(1)}, u32[]{:S(2)}, u32[]{:S(2)}) %all-to-all-start.5) | async-done | bytes 160 | tf_op jit(solution)/shard_map/all_to_all | solution.py:18
  350.5 1.3 broadcast_in_dim.49
  351.7 4.1 %all-to-all-start.7 = ((f32[32,1,1]{2,1,0:T(1,128)}), f32[32,1,1]{2,1,0:T(1,128)S(1)}, u32[]{:S(2)}, u32[]{:S(2)}) async-start(f32[32,1,1]{2,1,0:T(1,128)} %broadcast_in_dim.49), calls=%async_computation.7 | async-start | bytes 32768 | tf_op jit(solution)/shard_map/all_to_all | solution.py:18
  355.9 0.6 reduce_sum.145
  356.5 8.8 %all-to-all-done.7 = f32[32,1,1]{2,1,0:T(1,128)S(1)} async-done(((f32[32,1,1]{2,1,0:T(1,128)}), f32[32,1,1]{2,1,0:T(1,128)S(1)}, u32[]{:S(2)}, u32[]{:S(2)}) %all-to-all-start.7) | async-done | bytes 160 | tf_op jit(solution)/shard_map/all_to_all | solution.py:18
  365.3 0.6 reduce_sum.149
  367.4 0.7 copy.35
  368.0 0.7 multiply_add_fusion
  (55 shorter events, 6.8 us)
Async XLA Ops:
  7.2 34.5 %copy-start.5 = (s32[1,1,64]{2,1,0:T(1,128)S(1)}, s32[1,1,64]{2,1,0:T(1,128)}, u32[]{:S(2)}) copy-start(s32[1,1,64]{2,1,0:T(1,128)} %param.18) | copy-start | bytes 772
  7.2 101.4 %copy-start.1 = (f32[160,128]{1,0:T(8,128)S(1)}, f32[160,128]{1,0:T(8,128)}, u32[]{:S(2)}) copy-start(f32[160,128]{1,0:T(8,128)} %param.21) | copy-start | bytes 245764
  7.2 101.4 %copy-start = (f32[160,128]{1,0:T(8,128)S(1)}, f32[160,128]{1,0:T(8,128)}, u32[]{:S(2)}) copy-start(f32[160,128]{1,0:T(8,128)} %param.22) | copy-start | bytes 245764
  7.2 99.5 %all-gather.7.cloned.1.call-start = ((), (), s32[]{:S(2)}) async-start(), calls=%async_computation.8 | async-start | bytes 2703360 | tf_op jit(solution)/shard_map/all_gather | solution.py:13
  41.6 73.0 %copy-start.4 = (s32[1,1,64]{2,1,0:T(1,128)S(1)}, s32[1,1,64]{2,1,0:T(1,128)}, u32[]{:S(2)}) copy-start(s32[1,1,64]{2,1,0:T(1,128)} %param.19) | copy-start | bytes 772
  115.4 9.4 %all-to-all-start = ((f32[8,24,128]{2,1,0:T(8,128)}), f32[8,24,128]{2,1,0:T(8,128)S(1)}, u32[]{:S(2)}, u32[]{:S(2)}) async-start(f32[8,24,128]{2,1,0:T(8,128)} %broadcast_in_dim.42), calls=%async_computation | async-start | bytes 196608 | tf_op jit(solution)/shard_map/all_to_all | solution.py:18
  119.4 67.9 %all-gather.9.cloned.1.call-start = ((), (), s32[]{:S(2)}) async-start(), calls=%async_computation.9 | async-start | bytes 2703360 | tf_op jit(solution)/shard_map/all_gather | solution.py:13
  133.8 106.3 %copy-start.2 = (f32[160,128]{1,0:T(8,128)S(1)}, f32[160,128]{1,0:T(8,128)}, u32[]{:S(2)}) copy-start(f32[160,128]{1,0:T(8,128)} %param.24) | copy-start | bytes 245764
  133.8 106.3 %copy-start.3 = (f32[160,128]{1,0:T(8,128)S(1)}, f32[160,128]{1,0:T(8,128)}, u32[]{:S(2)}) copy-start(f32[160,128]{1,0:T(8,128)} %param.23) | copy-start | bytes 245764
  195.9 9.4 %all-to-all-start.2 = ((f32[8,24,128]{2,1,0:T(8,128)}), f32[8,24,128]{2,1,0:T(8,128)S(1)}, u32[]{:S(2)}, u32[]{:S(2)}) async-start(f32[8,24,128]{2,1,0:T(8,128)} %broadcast_in_dim.44), calls=%async_computation.2 | async-start | bytes 196608 | tf_op jit(solution)/shard_map/all_to_all | solution.py:18
  224.5 13.6 %all-to-all-start.3 = ((f32[32,1,1]{2,1,0:T(1,128)}), f32[32,1,1]{2,1,0:T(1,128)S(1)}, u32[]{:S(2)}, u32[]{:S(2)}) async-start(f32[32,1,1]{2,1,0:T(1,128)} %broadcast_in_dim.45), calls=%async_computation.3 | async-start | bytes 32768 | tf_op jit(solution)/shard_map/all_to_all | solution.py:18
  228.7 85.0 %all-gather.11.cloned.1.call-start = ((), (), s32[]{:S(2)}) async-start(), calls=%async_computation.10 | async-start | bytes 2703360 | tf_op jit(solution)/shard_map/all_gather | solution.py:13
  322.3 9.4 %all-to-all-start.6 = ((f32[8,24,128]{2,1,0:T(8,128)}), f32[8,24,128]{2,1,0:T(8,128)S(1)}, u32[]{:S(2)}, u32[]{:S(2)}) async-start(f32[8,24,128]{2,1,0:T(8,128)} %broadcast_in_dim.48), calls=%async_computation.6 | async-start | bytes 196608 | tf_op jit(solution)/shard_map/all_to_all | solution.py:18
  333.7 16.8 %all-to-all-start.5 = ((f32[32,1,1]{2,1,0:T(1,128)}), f32[32,1,1]{2,1,0:T(1,128)S(1)}, u32[]{:S(2)}, u32[]{:S(2)}) async-start(f32[32,1,1]{2,1,0:T(1,128)} %broadcast_in_dim.47), calls=%async_computation.5 | async-start | bytes 32768 | tf_op jit(solution)/shard_map/all_to_all | solution.py:18
  351.7 13.6 %all-to-all-start.7 = ((f32[32,1,1]{2,1,0:T(1,128)}), f32[32,1,1]{2,1,0:T(1,128)S(1)}, u32[]{:S(2)}, u32[]{:S(2)}) async-start(f32[32,1,1]{2,1,0:T(1,128)} %broadcast_in_dim.49), calls=%async_computation.7 | async-start | bytes 32768 | tf_op jit(solution)/shard_map/all_to_all | solution.py:18
Sparse Core Ops, SparseCore 0:
  42.6 64.0 all-gather.6
  134.7 52.4 all-gather.8
  264.0 49.5 all-gather.10
where the time goes:
time: 376 us; the launch traced here: 375 us
  waiting for transfers between devices  207 us (55%)
  matrix products  49.1 us (13%)
  blocking collectives  47.5 us (13%)
  starting transfers between devices  28 us (7%)
  between operations  18.6 us (5%)
  other arithmetic  13.1 us (3%)
  local copies, waits for them, and re-layouts  11.6 us (3%)
    all_gather x3, waiting for transfers between devices, total_of_pieces(): return lax.all_gather(array, axis).sum(0)  166 us
    all_to_all x6, waiting for transfers between devices, from_everyone(): return lax.all_to_all(copies, axis, split_axis=0, concat_axis=0, tiled=True)  41.4 us
    all_to_all x6, starting transfers between devices, from_everyone(): return lax.all_to_all(copies, axis, split_axis=0, concat_axis=0, tiled=True)  27.7 us
    dot_general x3, matrix products, forward_terms(): products = jnp.einsum('kij,kj->ki', flat_tiles, picked, precision=HIGH)  24.9 us
    all_to_all x2, blocking collectives, from_everyone(): return lax.all_to_all(copies, axis, split_axis=0, concat_axis=0, tiled=True)  24.4 us
    all_gather x1, blocking collectives, turned_gather(): out = lax.all_gather(both, axis, axis=0, tiled=True)  23 us
    dot_general x4, matrix products, apply_backward(): products = jnp.einsum('kij,ki->kj', flat_tiles, picked, precision=HIGH)  21.1 us
  transfers between devices with their start and end apart: 9, of which 9 were waited for; matrix products, arithmetic and copies ran while one was open for 0% of the time, Pallas kernels for 0%

commit v1 on v0

v1 whole, which is shorter than its diff:
```python
import functools

import jax
import jax.numpy as jnp
from jax import lax
from jax.experimental import pallas as pl
from jax.experimental.pallas import tpu as pltpu
from jax.sharding import PartitionSpec as P

ITERS = 2
MESH = pl.DeviceIdType.MESH
F32 = jnp.float32


def pieces(value, count):
    out = []
    for _ in range(count - 1):
        head = value.astype(jnp.bfloat16).astype(F32)
        out.append(head)
        value = value - head
    out.append(value)
    return out


def select(table, value, count):
    return sum(jnp.dot(table, part, preferred_element_type=F32) for part in pieces(value, count))


def kernel(
    dims,
    rho_ref,
    sigma_ref,
    relax_ref,
    rows_ref,
    cols_ref,
    x0_ref,
    diag0_ref,
    lin0_ref,
    z0_ref,
    y0_ref,
    low0_ref,
    high0_ref,
    tiles_hbm,
    x_out,
    z_out,
    y_out,
    tiles,
    turned,
    acc,
    row_pick,
    row_sum,
    col_pick,
    col_sum,
    zs,
    ys,
    low,
    high,
    image,
    xs,
    diag,
    lin,
    start_buf,
    back_buf,
    part_buf,
    rs_buf,
    ar_buf,
    ag_buf,
    srow_buf,
    scol_buf,
    load_sem,
    start_send,
    start_recv,
    back_send,
    back_recv,
    rs_send,
    rs_recv,
    ar_send,
    ar_recv,
    ag_send,
    ag_recv,
    srow_send,
    srow_recv,
    scol_send,
    scol_recv,
):
    n_row, n_hi, n_lo, xb, zb, pad, width = dims
    count = tiles.shape[0]
    lanes = tiles.shape[2]
    piece = zb // n_lo
    row = lax.axis_index("row")
    col = lax.axis_index("col")
    hi = lax.div(col, n_lo)
    lo = lax.rem(col, n_lo)

    def row_peer(step):
        other = lax.rem(row + step, n_row)
        return other, (other, col)

    def hi_peer(step):
        other = lax.rem(hi + step, n_hi)
        return other, (row, other * n_lo + lo)

    def lo_peer(step):
        other = lax.rem(lo + step, n_lo)
        return other, (row, hi * n_lo + other)

    groups = ((n_row, row_peer), (n_hi, hi_peer), (n_lo, lo_peer))

    barrier = pltpu.get_barrier_semaphore()
    for size, peer in groups:
        for step in range(1, size):
            pl.semaphore_signal(barrier, inc=1, device_id=peer(step)[1], device_id_type=MESH)

    load = pltpu.make_async_copy(tiles_hbm, tiles, load_sem)
    load.start()

    def exchange(size, peer, source, target, mine, send_sem, recv_sem):
        for step in range(1, size):
            other, device = peer(step)
            pltpu.make_async_remote_copy(
                src_ref=source(other),
                dst_ref=target(mine),
                send_sem=send_sem(other),
                recv_sem=recv_sem(mine),
                device_id=device,
                device_id_type=MESH,
            ).start()

    def arrive(size, peer, source, target, send_sem, recv_sem):
        for step in range(1, size):
            other, device = peer(step)
            copy = pltpu.make_async_remote_copy(
                src_ref=source(other),
                dst_ref=target(other),
                send_sem=send_sem(other),
                recv_sem=recv_sem(other),
                device_id=device,
                device_id_type=MESH,
            )
            copy.wait_recv()
            copy.wait_send()

    start_buf[row] = jnp.concatenate(
        [x0_ref[...], diag0_ref[...], lin0_ref[...], jnp.zeros((xb, lanes - 3 * width), F32)], axis=1
    )

    rows = rows_ref[...]
    padded = rows
    for k in range(1, n_lo):
        padded = padded + jnp.where(rows >= k * piece, pad - piece, 0)
    table = (lax.broadcasted_iota(jnp.int32, (n_lo * pad, count), 0) == padded).astype(F32)
    row_pick[...] = table.T
    spread = (
        lax.broadcasted_iota(jnp.int32, (count, 8 * count), 0)
        == lax.broadcasted_iota(jnp.int32, (count, 8 * count), 1) // 8
    ).astype(F32)
    row_sum[...] = jnp.dot(table, spread, preferred_element_type=F32)
    table = (lax.broadcasted_iota(jnp.int32, (xb, count), 0) == cols_ref[...]).astype(F32)
    col_pick[...] = table.T
    col_sum[...] = jnp.dot(table, spread, preferred_element_type=F32)

    pl.semaphore_wait(barrier, sum(size - 1 for size, _ in groups))

    start_args = (lambda other: start_buf.at[row], lambda slot: start_buf.at[slot])
    start_sems = (lambda k: start_send.at[k], lambda k: start_recv.at[k])
    exchange(n_row, row_peer, *start_args, row, *start_sems)

    for ref, source in ((zs, z0_ref), (ys, y0_ref), (low, low0_ref), (high, high0_ref)):
        ref[...] = jnp.zeros_like(ref)
        for k in range(n_lo):
            ref[k, 0:piece, :] = source[k * piece : (k + 1) * piece, :]

    load.wait()
    for k in range(count):
        turned[k] = tiles[k].T

    rho = rho_ref[0]
    sigma = sigma_ref[0]
    relax = relax_ref[0]

    def products(picked, which):
        columns = picked.T
        for k in range(count):
            terms = which[k] * columns[:, k : k + 1]
            acc[8 * k : 8 * k + 8, :] = jnp.sum(terms.reshape(lanes // 8, 8, lanes), axis=0)
        return acc[...]

    def forward(vector, scalars, turn):
        part = select(row_sum[...], products(select(col_pick[...], vector, 3), turned), 2)
        part_buf[turn] = part.reshape(n_lo, pad, lanes)
        for k, value in enumerate(scalars):
            for slot in range(n_lo):
                part_buf[turn, slot, piece + k : piece + k + 1, :] = value
        rs_buf[turn, lo] = part_buf[turn, lo]
        rs_args = (lambda other: part_buf.at[turn, other], lambda slot: rs_buf.at[turn, slot])
        rs_sems = (lambda k: rs_send.at[turn, k], lambda k: rs_recv.at[turn, k])
        exchange(n_lo, lo_peer, *rs_args, lo, *rs_sems)
        yield
        arrive(n_lo, lo_peer, *rs_args, *rs_sems)
        ar_buf[turn, hi] = sum(rs_buf[turn, k] for k in range(n_lo))
        ar_args = (lambda other: ar_buf.at[turn, hi], lambda slot: ar_buf.at[turn, slot])
        ar_sems = (lambda k: ar_send.at[turn, k], lambda k: ar_recv.at[turn, k])
        exchange(n_hi, hi_peer, *ar_args, hi, *ar_sems)
        yield
        arrive(n_hi, hi_peer, *ar_args, *ar_sems)
        whole = sum(ar_buf[turn, k] for k in range(n_hi))
        inside = lax.broadcasted_iota(jnp.int32, whole.shape, 0) < piece
        kept = jnp.where(inside, whole, 0.0)
        ag_buf[turn, lo] = kept
        ag_args = (lambda other: ag_buf.at[turn, lo], lambda slot: ag_buf.at[turn, slot])
        ag_sems = (lambda k: ag_send.at[turn, k], lambda k: ag_recv.at[turn, k])
        exchange(n_lo, lo_peer, *ag_args, lo, *ag_sems)
        yield kept, [whole[piece + k : piece + k + 1, :] for k in range(len(scalars))]
        arrive(n_lo, lo_peer, *ag_args, *ag_sems)
        yield

    arrive(n_row, row_peer, *start_args, *start_sems)
    lane = lax.broadcasted_iota(jnp.int32, (xb, lanes), 1)
    for index, ref in enumerate((xs, diag, lin)):
        total = jnp.zeros((xb, lanes), F32)
        for k in range(n_row):
            moved = pltpu.roll(start_buf[k], (width * (k - index)) % lanes, axis=1)
            total = jnp.where((lane >= width * k) & (lane < width * (k + 1)), moved, total)
        ref[...] = total

    for _ in forward(xs[...], [], 0):
        pass
    image[...] = ag_buf[0]

    def iteration(turn, carry):
        target = rho * zs[...] - ys[...] - rho * image[...]
        target = target.reshape(n_lo * pad, lanes)
        back_buf[turn, row] = select(col_sum[...], products(select(row_pick[...], target, 3), tiles), 2)
        back_args = (lambda other: back_buf.at[turn, row], lambda slot: back_buf.at[turn, slot])
        back_sems = (lambda k: back_send.at[turn, k], lambda k: back_recv.at[turn, k])
        exchange(n_row, row_peer, *back_args, row, *back_sems)
        local = -lin[...] - diag[...] * xs[...]
        arrive(n_row, row_peer, *back_args, *back_sems)
        residual = local + sum(back_buf[turn, k] for k in range(n_row))

        square = residual * residual
        norm = jnp.sum(square, axis=0, keepdims=True)
        bend = jnp.sum((diag[...] + sigma) * square, axis=0, keepdims=True)
        stages = forward(residual, [norm, bend], turn + 1)
        next(stages)
        next(stages)
        kept, (norm, bend) = next(stages)

        srow_buf[turn, row] = jnp.sum(kept * kept, axis=0, keepdims=True)
        srow_args = (lambda other: srow_buf.at[turn, row], lambda slot: srow_buf.at[turn, slot])
        srow_sems = (lambda k: srow_send.at[turn, k], lambda k: srow_recv.at[turn, k])
        exchange(n_row, row_peer, *srow_args, row, *srow_sems)
        arrive(n_row, row_peer, *srow_args, *srow_sems)
        scol_buf[turn, lo] = sum(srow_buf[turn, k] for k in range(n_row))
        scol_args = (lambda other: scol_buf.at[turn, lo], lambda slot: scol_buf.at[turn, slot])
        scol_sems = (lambda k: scol_send.at[turn, k], lambda k: scol_recv.at[turn, k])
        exchange(n_lo, lo_peer, *scol_args, lo, *scol_sems)
        next(stages)
        arrive(n_lo, lo_peer, *scol_args, *scol_sems)
        bend = bend + rho * sum(scol_buf[turn, k] for k in range(n_lo))

        step = jnp.sum(norm, axis=1, keepdims=True) / jnp.sum(bend, axis=1, keepdims=True)
        x_now = xs[...]
        xs[...] = relax * (x_now + step * residual) + (1.0 - relax) * x_now
        for k in range(n_lo):
            old = image[k]
            moved = old + step * ag_buf[turn + 1, k]
            image[k] = relax * moved + (1.0 - relax) * old
            mixed = relax * moved + (1.0 - relax) * zs[k]
            y_now = ys[k]
            z_new = jnp.minimum(jnp.maximum(mixed + y_now / rho, low[k]), high[k])
            ys[k] = y_now + rho * (mixed - z_new)
            zs[k] = z_new
        return carry

    lax.fori_loop(0, ITERS, iteration, 0)

    x_out[...] = pltpu.roll(xs[...], lax.rem(lanes - width * row, lanes), axis=1)[:, :width]
    for k in range(n_lo):
        z_out[k * piece : (k + 1) * piece, :] = zs[k, 0:piece, :]
        y_out[k * piece : (k + 1) * piece, :] = ys[k, 0:piece, :]


def solution(mesh):
    n_row, n_col = mesh.shape["row"], mesh.shape["col"]
    n_lo = 8
    n_hi = n_col // n_lo

    def shards(values, rows, cols, x0, z0, y0, low0, high0, diag0, lin0, rho, sigma, relax):
        order = values.shape[-1]
        tiles = values.reshape(-1, order, order)
        count = tiles.shape[0]
        zb, lanes = z0.shape
        xb, width = x0.shape
        piece = zb // n_lo
        pad = (piece + 2 + 7) // 8 * 8
        dims = (n_row, n_hi, n_lo, xb, zb, pad, width)
        smem = pl.BlockSpec(memory_space=pltpu.SMEM)
        vmem = pl.BlockSpec(memory_space=pltpu.VMEM)
        dma = pltpu.SemaphoreType.DMA
        wide = (n_lo, pad, lanes)
        return pl.pallas_call(
            functools.partial(kernel, dims),
            out_shape=(
                jax.ShapeDtypeStruct(x0.shape, F32),
                jax.ShapeDtypeStruct(z0.shape, F32),
                jax.ShapeDtypeStruct(z0.shape, F32),
            ),
            in_specs=[smem] * 3 + [vmem] * 9 + [pl.BlockSpec(memory_space=pl.ANY)],
            out_specs=(vmem, vmem, vmem),
            scratch_shapes=[
                pltpu.VMEM((count, order, order), F32),
                pltpu.VMEM((count, order, order), F32),
                pltpu.VMEM((8 * count, lanes), F32),
                pltpu.VMEM((count, n_lo * pad), F32),
                pltpu.VMEM((n_lo * pad, 8 * count), F32),
                pltpu.VMEM((count, xb), F32),
                pltpu.VMEM((xb, 8 * count), F32),
                *[pltpu.VMEM(wide, F32)] * 5,
                *[pltpu.VMEM((xb, lanes), F32)] * 3,
                pltpu.VMEM((n_row, xb, lanes), F32),
                pltpu.VMEM((ITERS, n_row, xb, lanes), F32),
                pltpu.VMEM((ITERS + 1, *wide), F32),
                pltpu.VMEM((ITERS + 1, *wide), F32),
                pltpu.VMEM((ITERS + 1, n_hi, pad, lanes), F32),
                pltpu.VMEM((ITERS + 1, *wide), F32),
                pltpu.VMEM((ITERS, n_row, 1, lanes), F32),
                pltpu.VMEM((ITERS, n_lo, 1, lanes), F32),
                dma(()),
                dma((n_row,)),
                dma((n_row,)),
                dma((ITERS, n_row)),
                dma((ITERS, n_row)),
                dma((ITERS + 1, n_lo)),
                dma((ITERS + 1, n_lo)),
                dma((ITERS + 1, n_hi)),
                dma((ITERS + 1, n_hi)),
                dma((ITERS + 1, n_lo)),
                dma((ITERS + 1, n_lo)),
                dma((ITERS, n_row)),
                dma((ITERS, n_row)),
                dma((ITERS, n_lo)),
                dma((ITERS, n_lo)),
            ],
            compiler_params=pltpu.CompilerParams(collective_id=0, has_side_effects=True),
            name="admm",
        )(rho, sigma, relax, rows.reshape(1, -1), cols.reshape(1, -1), x0, diag0, lin0, z0, y0, low0, high0, tiles)

    placed = (
        P("row", "col", None, None, None),
        P("row", "col", None),
        P("row", "col", None),
        P("col", "row"),
        P("row", None),
        P("row", None),
        P("row", None),
        P("row", None),
        P("col", "row"),
        P("col", "row"),
        P(),
        P(),
        P(),
    )
    return jax.shard_map(
        shards,
        mesh=mesh,
        in_specs=placed,
        out_specs=(P("col", "row"), P("row", None), P("row", None)),
        check_vma=False,
    )
```

time: 376 us -> 90.2 us (0.24)
  waiting for transfers between devices: 207 us -> 0 us
  Pallas kernels: 0 us -> 78.7 us
  matrix products: 49.1 us -> 0 us
  blocking collectives: 47.5 us -> 0 us
  starting transfers between devices: 28 us -> 0 us
  between operations: 18.6 us -> 2.58 us
  other arithmetic: 13.1 us -> 0 us
    all_gather x3 -> x0, waiting for transfers between devices: 166 us -> none  [total_of_pieces(): return lax.all_gather(array, axis).sum(0)]
    pallas_call x0 -> x1, Pallas kernels: none -> 78.7 us  [shards(): pl.pallas_call(functools.partial(kernel, dims), out_shape=(jax.ShapeDtype...]
    dot_general x14 -> x0, matrix products: 49.1 us -> none  [the longest x3 24.9 us: forward_terms(): products = jnp.einsum('kij,kj->ki', flat_tiles, picked, precision=HIGH)]
    all_to_all x6 -> x0, waiting for transfers between devices: 41.4 us -> none  [from_everyone(): return lax.all_to_all(copies, axis, split_axis=0, concat_axis=0, tiled=True)]
    all_to_all x6 -> x0, starting transfers between devices: 27.7 us -> none  [from_everyone(): return lax.all_to_all(copies, axis, split_axis=0, concat_axis=0, tiled=True)]
    all_to_all x2 -> x0, blocking collectives: 24.4 us -> none  [from_everyone(): return lax.all_to_all(copies, axis, split_axis=0, concat_axis=0, tiled=True)]
    all_gather x1 -> x0, blocking collectives: 23 us -> none  [turned_gather(): out = lax.all_gather(both, axis, axis=0, tiled=True)]
    reduce_sum x13 -> x0, other arithmetic: 9.53 us -> none  [the longest x3 5.64 us: total_of_pieces(): return lax.all_gather(array, axis).sum(0)]
  transfers between devices with their start and end apart: 9 -> 0, of which waited for: 9 -> 0; matrix products, arithmetic and copies ran while one was open for 0% -> 0% of each run, Pallas kernels for 0% -> 0%
where the time goes in v1:
time: 90.2 us; the launch traced here: 89.8 us
  Pallas kernels  78.7 us (87%)
  local copies, waits for them, and re-layouts  8.53 us (9%)
  between operations  2.58 us (3%)
    pallas_call x1, Pallas kernels, shards(): pl.pallas_call(functools.partial(kernel, dims), out_shape=(jax.ShapeDtype...  78.7 us
    unnamed x5, local copies, waits for them, and re-layouts  7.15 us

profile of v1, /device:TPU:1, one launch (start us, length us, event | category | flops | bytes accessed | tf_op | source)
XLA Modules:
  0.0 89.8 jit_solution(16786837227476673587)
XLA Ops:
  2.6 1.4 %copy.16.x0_ref = f32[24,16]{1,0:T(8,128)} copy(f32[24,16]{0,1:T(8,128)} %param.16) | data formatting | bytes 3072 | tf_op args[3]
  3.9 1.4 %copy.17.diag0_ref = f32[24,16]{1,0:T(8,128)} copy(f32[24,16]{0,1:T(8,128)} %param.21) | data formatting | bytes 3072 | tf_op args[8]
  5.3 1.4 %copy.18.lin0_ref = f32[24,16]{1,0:T(8,128)} copy(f32[24,16]{0,1:T(8,128)} %param.22) | data formatting | bytes 3072 | tf_op args[9]
  6.7 78.7 %admm.1 = (f32[24,16]{1,0:T(8,128)}, f32[160,128]{1,0:T(8,128)}, f32[160,128]{1,0:T(8,128)}) custom-call(f32[1]{0:T(128)S(6)} %copy.22.rho_ref, f32[1]{0:T(128)S(6)} %copy.23.sigma_ref, f32[1]{0:T(128)S(6)} %copy.24.relax_ref, s32[1,64]{1,0:T(1,128)} %bitcast.4, s32[1,64]{1,0:T(1,128)} %bitcast.5, f32[24,16]{1,0:T(8,128)} %copy.16.x0_ref, ...), custom_call_target="tpu_custom_call" | custom-call | tf_op jit(solution)/shard_map/admm/pallas_call | solution.py:302
  85.4 1.4 %copy.19 = f32[24,16]{0,1:T(8,128)} copy(f32[24,16]{1,0:T(8,128)} %get-tuple-element.3) | data formatting | bytes 3072 | tf_op jit(solution)/shard_map/admm/pallas_call | solution.py:302
  86.8 1.5 %copy.25 = f32[160,128]{1,0:T(8,128)} copy(f32[160,128]{1,0:T(8,128)} %get-tuple-element.10) | data formatting | bytes 163840
  88.3 1.5 %copy.26 = f32[160,128]{1,0:T(8,128)} copy(f32[160,128]{1,0:T(8,128)} %get-tuple-element.11) | data formatting | bytes 163840

commit v2 on v1

v2 whole, which is shorter than its diff:
```python
import functools

import jax
import jax.numpy as jnp
from jax import lax
from jax.experimental import pallas as pl
from jax.experimental.pallas import tpu as pltpu
from jax.sharding import PartitionSpec as P

ITERS = 2
MESH = pl.DeviceIdType.MESH
F32 = jnp.float32
BF16 = jnp.bfloat16


def pieces(value, count):
    out = []
    for _ in range(count - 1):
        head = value.astype(BF16)
        out.append(head)
        value = value - head.astype(F32)
    out.append(value.astype(BF16))
    return out


def select(table, value):
    return sum(jnp.dot(table, part, preferred_element_type=F32) for part in pieces(value, 2))


def kernel(
    dims,
    rho_hbm,
    sigma_hbm,
    relax_hbm,
    rows_hbm,
    cols_hbm,
    x0_hbm,
    diag0_hbm,
    lin0_hbm,
    z0_hbm,
    y0_hbm,
    low0_hbm,
    high0_hbm,
    tiles_hbm,
    out,
    rho_ref,
    sigma_ref,
    relax_ref,
    rows_ref,
    cols_ref,
    index_buf,
    small_buf,
    plain_buf,
    tiles,
    turned,
    acc,
    picked,
    vector_buf,
    row_sum,
    col_sum,
    zs,
    ys,
    low,
    high,
    image,
    xs,
    diag,
    lin,
    start_buf,
    cost_buf,
    back_buf,
    part_buf,
    rs_buf,
    ar_buf,
    ag_buf,
    norm_buf,
    load_sem,
    start_send,
    start_recv,
    cost_send,
    cost_recv,
    back_send,
    back_recv,
    rs_send,
    rs_recv,
    ar_send,
    ar_recv,
    ag_send,
    ag_recv,
    norm_send,
    norm_recv,
):
    n_row, n_hi, n_lo, xb, zb, pad, width = dims
    count = tiles.shape[0]
    lanes = tiles.shape[2]
    piece = zb // n_lo
    row = lax.axis_index("row")
    col = lax.axis_index("col")
    hi = lax.div(col, n_lo)
    lo = lax.rem(col, n_lo)

    def row_peer(step):
        other = lax.rem(row + step, n_row)
        return other, (other, col)

    def hi_peer(step):
        other = lax.rem(hi + step, n_hi)
        return other, (row, other * n_lo + lo)

    def lo_peer(step):
        other = lax.rem(lo + step, n_lo)
        return other, (row, hi * n_lo + other)

    def plane_peer(step):
        other_row = lax.rem(row + step // n_lo, n_row)
        other_lo = lax.rem(lo + step % n_lo, n_lo)
        return other_row * n_lo + other_lo, (other_row, hi * n_lo + other_lo)

    n_plane = n_row * n_lo
    plane = row * n_lo + lo

    barrier = pltpu.get_barrier_semaphore()
    for size, peer in ((n_plane, plane_peer), (n_hi, hi_peer)):
        for step in range(1, size):
            pl.semaphore_signal(barrier, inc=1, device_id=peer(step)[1], device_id_type=MESH)

    loads = [
        pltpu.make_async_copy(source, target, load_sem.at[k])
        for k, (source, target) in enumerate(
            (
                (x0_hbm, small_buf.at[0]),
                (diag0_hbm, small_buf.at[1]),
                (lin0_hbm, small_buf.at[2]),
                (rows_hbm, index_buf.at[0]),
                (cols_hbm, index_buf.at[1]),
                (rows_hbm, rows_ref),
                (cols_hbm, cols_ref),
                (rho_hbm, rho_ref),
                (sigma_hbm, sigma_ref),
                (relax_hbm, relax_ref),
                (z0_hbm, plain_buf.at[0]),
                (y0_hbm, plain_buf.at[1]),
                (low0_hbm, plain_buf.at[2]),
                (high0_hbm, plain_buf.at[3]),
                (tiles_hbm, tiles),
            )
        )
    ]
    for load in loads:
        load.start()

    def exchange(size, peer, source, target, mine, send_sem, recv_sem):
        for step in range(1, size):
            other, device = peer(step)
            pltpu.make_async_remote_copy(
                src_ref=source(other),
                dst_ref=target(mine),
                send_sem=send_sem(other),
                recv_sem=recv_sem(mine),
                device_id=device,
                device_id_type=MESH,
            ).start()

    def arrive(size, peer, source, target, send_sem, recv_sem):
        for step in range(1, size):
            other, device = peer(step)
            copy = pltpu.make_async_remote_copy(
                src_ref=source(other),
                dst_ref=target(other),
                send_sem=send_sem(other),
                recv_sem=recv_sem(other),
                device_id=device,
                device_id_type=MESH,
            )
            copy.wait_recv()
            copy.wait_send()

    empty = jnp.zeros((width, lanes - xb), F32)
    for load in loads[:5]:
        load.wait()
    start_buf[row] = jnp.concatenate([small_buf[0], empty], axis=1)
    for k in range(2):
        cost_buf[row, k] = jnp.concatenate([small_buf[k + 1], empty], axis=1)

    rows = index_buf[0]
    padded = rows
    for k in range(1, n_lo):
        padded = padded + jnp.where(rows >= k * piece, pad - piece, 0)
    row_sum[...] = (lax.broadcasted_iota(jnp.int32, (n_lo * pad, count), 0) == padded).astype(BF16)
    col_sum[...] = (lax.broadcasted_iota(jnp.int32, (xb, count), 0) == index_buf[1]).astype(BF16)
    for load in loads[5:10]:
        load.wait()

    pl.semaphore_wait(barrier, n_plane - 1 + n_hi - 1)

    start_args = (lambda other: start_buf.at[row], lambda slot: start_buf.at[slot])
    start_sems = (lambda k: start_send.at[k], lambda k: start_recv.at[k])
    exchange(n_row, row_peer, *start_args, row, *start_sems)
    cost_args = (lambda other: cost_buf.at[row], lambda slot: cost_buf.at[slot])
    cost_sems = (lambda k: cost_send.at[k], lambda k: cost_recv.at[k])
    exchange(n_row, row_peer, *cost_args, row, *cost_sems)

    for load in loads[10:]:
        load.wait()
    for k in range(count):
        turned[k] = tiles[k].T
    for index, ref in enumerate((zs, ys, low, high)):
        ref[...] = jnp.zeros_like(ref)
        for k in range(n_lo):
            ref[k, 0:piece, :] = plain_buf[index, k * piece : (k + 1) * piece, :]

    rho = rho_ref[0]
    sigma = sigma_ref[0]
    relax = relax_ref[0]

    def products(which):
        columns = picked[...].T
        for k in range(count):
            terms = which[k] * columns[:, k : k + 1]
            acc[k : k + 1, :] = jnp.sum(terms, axis=0, keepdims=True)
        return acc[...]

    def forward(vector, scalars, turn):
        vector_buf[0:xb, :] = vector
        for k in range(count):
            picked[k : k + 1, :] = vector_buf[pl.ds(cols_ref[0, k], 1), :]
        part = select(row_sum[...], products(turned))
        part_buf[turn] = part.reshape(n_lo, pad, lanes)
        for k, value in enumerate(scalars):
            for slot in range(n_lo):
                part_buf[turn, slot, piece + k : piece + k + 1, :] = value
        rs_buf[turn, lo] = part_buf[turn, lo]
        rs_args = (lambda other: part_buf.at[turn, other], lambda slot: rs_buf.at[turn, slot])
        rs_sems = (lambda k: rs_send.at[turn, k], lambda k: rs_recv.at[turn, k])
        exchange(n_lo, lo_peer, *rs_args, lo, *rs_sems)
        yield
        arrive(n_lo, lo_peer, *rs_args, *rs_sems)
        ar_buf[turn, hi] = sum(rs_buf[turn, k] for k in range(n_lo))
        ar_args = (lambda other: ar_buf.at[turn, hi], lambda slot: ar_buf.at[turn, slot])
        ar_sems = (lambda k: ar_send.at[turn, k], lambda k: ar_recv.at[turn, k])
        exchange(n_hi, hi_peer, *ar_args, hi, *ar_sems)
        yield
        arrive(n_hi, hi_peer, *ar_args, *ar_sems)
        whole = sum(ar_buf[turn, k] for k in range(n_hi))
        inside = lax.broadcasted_iota(jnp.int32, whole.shape, 0) < piece
        kept = jnp.where(inside, whole, 0.0)
        ag_buf[turn, lo] = kept
        ag_args = (lambda other: ag_buf.at[turn, lo], lambda slot: ag_buf.at[turn, slot])
        ag_sems = (lambda k: ag_send.at[turn, k], lambda k: ag_recv.at[turn, k])
        if scalars:
            norm_buf[turn - 1, plane] = jnp.sum(kept * kept, axis=0, keepdims=True)
            exchange(n_plane, plane_peer, *norm_args(turn - 1), plane, *norm_sems(turn - 1))
        exchange(n_lo, lo_peer, *ag_args, lo, *ag_sems)
        yield [whole[piece + k : piece + k + 1, :] for k in range(len(scalars))]
        arrive(n_lo, lo_peer, *ag_args, *ag_sems)
        yield

    def norm_args(turn):
        return lambda other: norm_buf.at[turn, plane], lambda slot: norm_buf.at[turn, slot]

    def norm_sems(turn):
        return lambda k: norm_send.at[turn, k], lambda k: norm_recv.at[turn, k]

    arrive(n_row, row_peer, *start_args, *start_sems)
    xs[...] = jnp.concatenate([start_buf[k] for k in range(n_row)], axis=0).T[:xb]
    stages = forward(xs[...], [], 0)
    next(stages)
    arrive(n_row, row_peer, *cost_args, *cost_sems)
    diag[...] = jnp.concatenate([cost_buf[k, 0] for k in range(n_row)], axis=0).T[:xb]
    lin[...] = jnp.concatenate([cost_buf[k, 1] for k in range(n_row)], axis=0).T[:xb]
    for _ in stages:
        pass
    image[...] = ag_buf[0]

    def iteration(turn, carry):
        for k in range(n_lo):
            vector_buf[k * pad : (k + 1) * pad, :] = rho * zs[k] - ys[k] - rho * image[k]
        for k in range(count):
            index = rows_ref[0, k]
            index = index + (pad - piece) * (index // piece)
            picked[k : k + 1, :] = vector_buf[pl.ds(index, 1), :]
        back_buf[turn, row] = select(col_sum[...], products(tiles))
        back_args = (lambda other: back_buf.at[turn, row], lambda slot: back_buf.at[turn, slot])
        back_sems = (lambda k: back_send.at[turn, k], lambda k: back_recv.at[turn, k])
        exchange(n_row, row_peer, *back_args, row, *back_sems)
        local = -lin[...] - diag[...] * xs[...]
        arrive(n_row, row_peer, *back_args, *back_sems)
        residual = local + sum(back_buf[turn, k] for k in range(n_row))

        square = residual * residual
        norm = jnp.sum(square, axis=0, keepdims=True)
        bend = jnp.sum((diag[...] + sigma) * square, axis=0, keepdims=True)
        stages = forward(residual, [norm, bend], turn + 1)
        next(stages)
        next(stages)
        norm, bend = next(stages)
        next(stages)
        arrive(n_plane, plane_peer, *norm_args(turn), *norm_sems(turn))
        bend = bend + rho * jnp.sum(norm_buf[turn], axis=0)

        step = jnp.sum(norm, axis=1, keepdims=True) / jnp.sum(bend, axis=1, keepdims=True)
        x_now = xs[...]
        xs[...] = relax * (x_now + step * residual) + (1.0 - relax) * x_now
        for k in range(n_lo):
            old = image[k]
            moved = old + step * ag_buf[turn + 1, k]
            image[k] = relax * moved + (1.0 - relax) * old
            mixed = relax * moved + (1.0 - relax) * zs[k]
            y_now = ys[k]
            z_new = jnp.minimum(jnp.maximum(mixed + y_now / rho, low[k]), high[k])
            ys[k] = y_now + rho * (mixed - z_new)
            zs[k] = z_new
        return carry

    lax.fori_loop(0, ITERS, iteration, 0)

    for k in range(n_lo):
        out[k * piece : (k + 1) * piece, :] = zs[k, 0:piece, :]
        out[zb + k * piece : zb + (k + 1) * piece, :] = ys[k, 0:piece, :]
    mine = pltpu.roll(xs[...], lax.rem(lanes - width * row, lanes), axis=1)
    out[2 * zb : 2 * zb + xb, :] = mine


def unpack(packed, x_out, z_out, y_out):
    zb = z_out.shape[0]
    width, xb = x_out.shape
    z_out[...] = packed[0:zb, :]
    y_out[...] = packed[zb : 2 * zb, :]
    x_out[...] = packed[2 * zb : 2 * zb + xb, :].T[:width]


def solution(mesh):
    n_row, n_col = mesh.shape["row"], mesh.shape["col"]
    n_lo = 8
    n_hi = n_col // n_lo

    def shards(values, rows, cols, x0, z0, y0, low0, high0, diag0, lin0, rho, sigma, relax):
        order = values.shape[-1]
        tiles = values.reshape(-1, order, order)
        count = tiles.shape[0]
        zb, lanes = z0.shape
        xb, width = x0.shape
        piece = zb // n_lo
        pad = (piece + 2 + 7) // 8 * 8
        dims = (n_row, n_hi, n_lo, xb, zb, pad, width)
        smem = pltpu.SMEM
        vmem = pltpu.VMEM
        dma = pltpu.SemaphoreType.DMA
        wide = (n_lo, pad, lanes)
        packed = pl.pallas_call(
            functools.partial(kernel, dims),
            out_shape=jax.ShapeDtypeStruct((2 * zb + xb, lanes), F32),
            in_specs=[pl.BlockSpec(memory_space=pltpu.HBM)] * 13,
            out_specs=pl.BlockSpec(memory_space=pltpu.VMEM),
            scratch_shapes=[
                smem((1,), F32),
                smem((1,), F32),
                smem((1,), F32),
                smem((1, count), jnp.int32),
                smem((1, count), jnp.int32),
                vmem((2, 1, count), jnp.int32),
                vmem((3, width, xb), F32),
                vmem((4, zb, lanes), F32),
                vmem((count, order, order), F32),
                vmem((count, order, order), F32),
                vmem((count, lanes), F32),
                vmem((count, lanes), F32),
                vmem((n_lo * pad, lanes), F32),
                vmem((n_lo * pad, count), BF16),
                vmem((xb, count), BF16),
                *[vmem(wide, F32)] * 5,
                *[vmem((xb, lanes), F32)] * 3,
                vmem((n_row, width, lanes), F32),
                vmem((n_row, 2, width, lanes), F32),
                vmem((ITERS, n_row, xb, lanes), F32),
                vmem((ITERS + 1, *wide), F32),
                vmem((ITERS + 1, *wide), F32),
                vmem((ITERS + 1, n_hi, pad, lanes), F32),
                vmem((ITERS + 1, *wide), F32),
                vmem((ITERS, n_row * n_lo, 1, lanes), F32),
                dma((15,)),
                dma((n_row,)),
                dma((n_row,)),
                dma((n_row,)),
                dma((n_row,)),
                dma((ITERS, n_row)),
                dma((ITERS, n_row)),
                dma((ITERS + 1, n_lo)),
                dma((ITERS + 1, n_lo)),
                dma((ITERS + 1, n_hi)),
                dma((ITERS + 1, n_hi)),
                dma((ITERS + 1, n_lo)),
                dma((ITERS + 1, n_lo)),
                dma((ITERS, n_row * n_lo)),
                dma((ITERS, n_row * n_lo)),
            ],
            compiler_params=pltpu.CompilerParams(collective_id=0, has_side_effects=True),
            name="admm",
        )(
            rho, sigma, relax, rows.reshape(1, -1), cols.reshape(1, -1),
            x0.T, diag0.T, lin0.T, z0, y0, low0, high0, tiles,
        )
        x_new, z_new, y_new = pl.pallas_call(
            unpack,
            out_shape=(
                jax.ShapeDtypeStruct((width, xb), F32),
                jax.ShapeDtypeStruct((zb, lanes), F32),
                jax.ShapeDtypeStruct((zb, lanes), F32),
            ),
            name="unpack",
        )(packed)
        return x_new.T, z_new, y_new

    placed = (
        P("row", "col", None, None, None),
        P("row", "col", None),
        P("row", "col", None),
        P("col", "row"),
        P("row", None),
        P("row", None),
        P("row", None),
        P("row", None),
        P("col", "row"),
        P("col", "row"),
        P(),
        P(),
        P(),
    )
    return jax.shard_map(
        shards,
        mesh=mesh,
        in_specs=placed,
        out_specs=(P("col", "row"), P("row", None), P("row", None)),
        check_vma=False,
    )
```

time: 90.2 us -> 82.3 us (0.912)
  local copies, waits for them, and re-layouts: 8.53 us -> 0 us
    unnamed x5 -> x0, local copies, waits for them, and re-layouts: 7.15 us -> none
    pallas_call x1 -> x0, local copies, waits for them, and re-layouts: 1.38 us -> none  [shards(): pl.pallas_call(functools.partial(kernel, dims), out_shape=(jax.ShapeDtype...]
    pallas_call x1 -> x2, Pallas kernels: 78.7 us -> 79.6 us  [the longest x1 78 us: shards(): pl.pallas_call(functools.partial(kernel, dims), out_shape=jax.ShapeDtypeS...]
where the time goes in v2:
time: 82.3 us; the launch traced here: 82.1 us
  Pallas kernels  79.6 us (97%)
  between operations  2.58 us (3%)
    pallas_call x1, Pallas kernels, shards(): pl.pallas_call(functools.partial(kernel, dims), out_shape=jax.ShapeDtypeS...  78 us

profile of v2, /device:TPU:1, one launch (start us, length us, event | category | flops | bytes accessed | tf_op | source)
XLA Modules:
  0.0 82.1 jit_solution(6235608673967155554)
XLA Ops:
  2.6 78.0 %admm.1.packed = f32[344,128]{1,0:T(8,128)} custom-call(f32[1]{0:T(128)S(6)} %copy.16.rho_hbm, f32[1]{0:T(128)S(6)} %copy.17.sigma_hbm, f32[1]{0:T(128)S(6)} %copy.18.relax_hbm, s32[1,64]{1,0:T(1,128)} %bitcast.11, s32[1,64]{1,0:T(1,128)} %bitcast.12, f32[16,24]{1,0:T(8,128)} %bitcast.8, f32[16,24]{1,0:T(8,128)} %bitcast.9, f32[16,24]{1,0:T(8,128)} %bitcast.10, ...), custom_call_target="tpu_custom_call" | custom-call | tf_op jit(solution)/shard_map/admm/pallas_call | solution.py:350
  80.6 1.6 %unpack.1 = (f32[16,24]{1,0:T(8,128)}, f32[160,128]{1,0:T(8,128)}, f32[160,128]{1,0:T(8,128)}) custom-call(f32[344,128]{1,0:T(8,128)} %admm.1.packed), custom_call_target="tpu_custom_call" | custom-call | tf_op jit(solution)/shard_map/unpack/pallas_call | solution.py:403

commit v3 on v2

--- a/solution.py
+++ b/solution.py
@@ -29,9 +29,9 @@
 
 def kernel(
     dims,
-    rho_hbm,
-    sigma_hbm,
-    relax_hbm,
+    rho_ref,
+    sigma_ref,
+    relax_ref,
     rows_hbm,
     cols_hbm,
     x0_hbm,
@@ -43,9 +43,6 @@
     high0_hbm,
     tiles_hbm,
     out,
-    rho_ref,
-    sigma_ref,
-    relax_ref,
     rows_ref,
     cols_ref,
     index_buf,
@@ -124,60 +121,43 @@
         for step in range(1, size):
             pl.semaphore_signal(barrier, inc=1, device_id=peer(step)[1], device_id_type=MESH)
 
-    loads = [
-        pltpu.make_async_copy(source, target, load_sem.at[k])
-        for k, (source, target) in enumerate(
-            (
-                (x0_hbm, small_buf.at[0]),
-                (diag0_hbm, small_buf.at[1]),
-                (lin0_hbm, small_buf.at[2]),
-                (rows_hbm, index_buf.at[0]),
-                (cols_hbm, index_buf.at[1]),
-                (rows_hbm, rows_ref),
-                (cols_hbm, cols_ref),
-                (rho_hbm, rho_ref),
-                (sigma_hbm, sigma_ref),
-                (relax_hbm, relax_ref),
-                (z0_hbm, plain_buf.at[0]),
-                (y0_hbm, plain_buf.at[1]),
-                (low0_hbm, plain_buf.at[2]),
-                (high0_hbm, plain_buf.at[3]),
-                (tiles_hbm, tiles),
-            )
-        )
-    ]
-    for load in loads:
-        load.start()
-
-    def exchange(size, peer, source, target, mine, send_sem, recv_sem):
+    smalls = [(x0_hbm, small_buf.at[0], 0), (diag0_hbm, small_buf.at[1], 0), (lin0_hbm, small_buf.at[2], 0)]
+    indices = [(rows_hbm, index_buf.at[0], 1), (cols_hbm, index_buf.at[1], 1), (rows_hbm, rows_ref, 2), (cols_hbm, cols_ref, 3)]
+    plains = [(ref, plain_buf.at[k], 4) for k, ref in enumerate((z0_hbm, y0_hbm, low0_hbm, high0_hbm))]
+    for source, target, k in [*smalls, *indices, *plains, (tiles_hbm, tiles, 5)]:
+        pltpu.make_async_copy(source, target, load_sem.at[k]).start()
+
+    def loaded(k, target):
+        pltpu.make_async_copy(target, target, load_sem.at[k]).wait()
+
+    def exchange(size, peer, source, buffer, mine, send_sem, recv_sem):
         for step in range(1, size):
             other, device = peer(step)
             pltpu.make_async_remote_copy(
                 src_ref=source(other),
-                dst_ref=target(mine),
-                send_sem=send_sem(other),
-                recv_sem=recv_sem(mine),
+                dst_ref=buffer.at[mine],
+                send_sem=send_sem,
+                recv_sem=recv_sem,
                 device_id=device,
                 device_id_type=MESH,
             ).start()
 
-    def arrive(size, peer, source, target, send_sem, recv_sem):
-        for step in range(1, size):
-            other, device = peer(step)
-            copy = pltpu.make_async_remote_copy(
-                src_ref=source(other),
-                dst_ref=target(other),
-                send_sem=send_sem(other),
-                recv_sem=recv_sem(other),
-                device_id=device,
-                device_id_type=MESH,
-            )
-            copy.wait_recv()
-            copy.wait_send()
+    def arrive(size, peer, source, buffer, mine, send_sem, recv_sem):
+        every = buffer.at[pl.ds(0, size - 1)]
+        copies = pltpu.make_async_remote_copy(
+            src_ref=every,
+            dst_ref=every,
+            send_sem=send_sem,
+            recv_sem=recv_sem,
+            device_id=peer(1)[1],
+            device_id_type=MESH,
+        )
+        copies.wait_recv()
+        copies.wait_send()
 
     empty = jnp.zeros((width, lanes - xb), F32)
-    for load in loads[:5]:
-        load.wait()
+    loaded(0, small_buf)
+    loaded(1, index_buf)
     start_buf[row] = jnp.concatenate([small_buf[0], empty], axis=1)
     for k in range(2):
         cost_buf[row, k] = jnp.concatenate([small_buf[k + 1], empty], axis=1)
@@ -188,20 +168,18 @@
         padded = padded + jnp.where(rows >= k * piece, pad - piece, 0)
     row_sum[...] = (lax.broadcasted_iota(jnp.int32, (n_lo * pad, count), 0) == padded).astype(BF16)
     col_sum[...] = (lax.broadcasted_iota(jnp.int32, (xb, count), 0) == index_buf[1]).astype(BF16)
-    for load in loads[5:10]:
-        load.wait()
+    loaded(2, rows_ref)
+    loaded(3, cols_ref)
 
     pl.semaphore_wait(barrier, n_plane - 1 + n_hi - 1)
 
-    start_args = (lambda other: start_buf.at[row], lambda slot: start_buf.at[slot])
-    start_sems = (lambda k: start_send.at[k], lambda k: start_recv.at[k])
-    exchange(n_row, row_peer, *start_args, row, *start_sems)
-    cost_args = (lambda other: cost_buf.at[row], lambda slot: cost_buf.at[slot])
-    cost_sems = (lambda k: cost_send.at[k], lambda k: cost_recv.at[k])
-    exchange(n_row, row_peer, *cost_args, row, *cost_sems)
-
-    for load in loads[10:]:
-        load.wait()
+    start = (n_row, row_peer, lambda other: start_buf.at[row], start_buf, row, start_send, start_recv)
+    exchange(*start)
+    cost = (n_row, row_peer, lambda other: cost_buf.at[row], cost_buf, row, cost_send, cost_recv)
+    exchange(*cost)
+
+    loaded(4, plain_buf)
+    loaded(5, tiles)
     for k in range(count):
         turned[k] = tiles[k].T
     for index, ref in enumerate((zs, ys, low, high)):
@@ -230,42 +208,40 @@
             for slot in range(n_lo):
                 part_buf[turn, slot, piece + k : piece + k + 1, :] = value
         rs_buf[turn, lo] = part_buf[turn, lo]
-        rs_args = (lambda other: part_buf.at[turn, other], lambda slot: rs_buf.at[turn, slot])
-        rs_sems = (lambda k: rs_send.at[turn, k], lambda k: rs_recv.at[turn, k])
-        exchange(n_lo, lo_peer, *rs_args, lo, *rs_sems)
+        parts = part_buf.at[turn]
+        scatter = (n_lo, lo_peer, lambda other: parts.at[other], rs_buf.at[turn], lo, rs_send.at[turn], rs_recv.at[turn])
+        exchange(*scatter)
         yield
-        arrive(n_lo, lo_peer, *rs_args, *rs_sems)
+        arrive(*scatter)
         ar_buf[turn, hi] = sum(rs_buf[turn, k] for k in range(n_lo))
-        ar_args = (lambda other: ar_buf.at[turn, hi], lambda slot: ar_buf.at[turn, slot])
-        ar_sems = (lambda k: ar_send.at[turn, k], lambda k: ar_recv.at[turn, k])
-        exchange(n_hi, hi_peer, *ar_args, hi, *ar_sems)
+        sums = ar_buf.at[turn]
+        reduce = (n_hi, hi_peer, lambda other: sums.at[hi], sums, hi, ar_send.at[turn], ar_recv.at[turn])
+        exchange(*reduce)
         yield
-        arrive(n_hi, hi_peer, *ar_args, *ar_sems)
+        arrive(*reduce)
         whole = sum(ar_buf[turn, k] for k in range(n_hi))
         inside = lax.broadcasted_iota(jnp.int32, whole.shape, 0) < piece
         kept = jnp.where(inside, whole, 0.0)
         ag_buf[turn, lo] = kept
-        ag_args = (lambda other: ag_buf.at[turn, lo], lambda slot: ag_buf.at[turn, slot])
-        ag_sems = (lambda k: ag_send.at[turn, k], lambda k: ag_recv.at[turn, k])
+        wholes = ag_buf.at[turn]
+        gather = (n_lo, lo_peer, lambda other: wholes.at[lo], wholes, lo, ag_send.at[turn], ag_recv.at[turn])
+        exchange(*gather)
         if scalars:
             norm_buf[turn - 1, plane] = jnp.sum(kept * kept, axis=0, keepdims=True)
-            exchange(n_plane, plane_peer, *norm_args(turn - 1), plane, *norm_sems(turn - 1))
-        exchange(n_lo, lo_peer, *ag_args, lo, *ag_sems)
+            exchange(*norms(turn - 1))
         yield [whole[piece + k : piece + k + 1, :] for k in range(len(scalars))]
-        arrive(n_lo, lo_peer, *ag_args, *ag_sems)
+        arrive(*gather)
         yield
 
-    def norm_args(turn):
-        return lambda other: norm_buf.at[turn, plane], lambda slot: norm_buf.at[turn, slot]
-
-    def norm_sems(turn):
-        return lambda k: norm_send.at[turn, k], lambda k: norm_recv.at[turn, k]
-
-    arrive(n_row, row_peer, *start_args, *start_sems)
+    def norms(turn):
+        buffer = norm_buf.at[turn]
+        return n_plane, plane_peer, lambda other: buffer.at[plane], buffer, plane, norm_send.at[turn], norm_recv.at[turn]
+
+    arrive(*start)
     xs[...] = jnp.concatenate([start_buf[k] for k in range(n_row)], axis=0).T[:xb]
     stages = forward(xs[...], [], 0)
     next(stages)
-    arrive(n_row, row_peer, *cost_args, *cost_sems)
+    arrive(*cost)
     diag[...] = jnp.concatenate([cost_buf[k, 0] for k in range(n_row)], axis=0).T[:xb]
     lin[...] = jnp.concatenate([cost_buf[k, 1] for k in range(n_row)], axis=0).T[:xb]
     for _ in stages:
@@ -280,11 +256,11 @@
             index = index + (pad - piece) * (index // piece)
             picked[k : k + 1, :] = vector_buf[pl.ds(index, 1), :]
         back_buf[turn, row] = select(col_sum[...], products(tiles))
-        back_args = (lambda other: back_buf.at[turn, row], lambda slot: back_buf.at[turn, slot])
-        back_sems = (lambda k: back_send.at[turn, k], lambda k: back_recv.at[turn, k])
-        exchange(n_row, row_peer, *back_args, row, *back_sems)
+        backs = back_buf.at[turn]
+        back = (n_row, row_peer, lambda other: backs.at[row], backs, row, back_send.at[turn], back_recv.at[turn])
+        exchange(*back)
         local = -lin[...] - diag[...] * xs[...]
-        arrive(n_row, row_peer, *back_args, *back_sems)
+        arrive(*back)
         residual = local + sum(back_buf[turn, k] for k in range(n_row))
 
         square = residual * residual
@@ -295,7 +271,7 @@
         next(stages)
         norm, bend = next(stages)
         next(stages)
-        arrive(n_plane, plane_peer, *norm_args(turn), *norm_sems(turn))
+        arrive(*norms(turn))
         bend = bend + rho * jnp.sum(norm_buf[turn], axis=0)
 
         step = jnp.sum(norm, axis=1, keepdims=True) / jnp.sum(bend, axis=1, keepdims=True)
@@ -318,15 +294,24 @@
         out[k * piece : (k + 1) * piece, :] = zs[k, 0:piece, :]
         out[zb + k * piece : zb + (k + 1) * piece, :] = ys[k, 0:piece, :]
     mine = pltpu.roll(xs[...], lax.rem(lanes - width * row, lanes), axis=1)
-    out[2 * zb : 2 * zb + xb, :] = mine
-
-
-def unpack(packed, x_out, z_out, y_out):
+    mine = jnp.concatenate([mine, jnp.zeros((lanes - xb, lanes), F32)], axis=0)
+    out[2 * zb : 2 * zb + width, :] = mine.T[:width]
+
+
+def unpack(packed, x_out, z_out, y_out, x_buf, sems):
     zb = z_out.shape[0]
     width, xb = x_out.shape
-    z_out[...] = packed[0:zb, :]
-    y_out[...] = packed[zb : 2 * zb, :]
-    x_out[...] = packed[2 * zb : 2 * zb + xb, :].T[:width]
+    copies = (
+        pltpu.make_async_copy(packed.at[pl.ds(0, zb)], z_out, sems.at[0]),
+        pltpu.make_async_copy(packed.at[pl.ds(zb, zb)], y_out, sems.at[1]),
+        pltpu.make_async_copy(x_buf, x_out, sems.at[2]),
+    )
+    copies[0].start()
+    copies[1].start()
+    x_buf[...] = packed[2 * zb : 2 * zb + width, :xb]
+    copies[2].start()
+    for copy in copies:
+        copy.wait()
 
 
 def solution(mesh):
@@ -349,13 +334,10 @@
         wide = (n_lo, pad, lanes)
         packed = pl.pallas_call(
             functools.partial(kernel, dims),
-            out_shape=jax.ShapeDtypeStruct((2 * zb + xb, lanes), F32),
-            in_specs=[pl.BlockSpec(memory_space=pltpu.HBM)] * 13,
+            out_shape=vmem((2 * zb + width, lanes), F32),
+            in_specs=[pl.BlockSpec(memory_space=smem)] * 3 + [pl.BlockSpec(memory_space=pl.ANY)] * 10,
             out_specs=pl.BlockSpec(memory_space=pltpu.VMEM),
             scratch_shapes=[
-                smem((1,), F32),
-                smem((1,), F32),
-                smem((1,), F32),
                 smem((1, count), jnp.int32),
                 smem((1, count), jnp.int32),
                 vmem((2, 1, count), jnp.int32),
@@ -378,21 +360,16 @@
                 vmem((ITERS + 1, n_hi, pad, lanes), F32),
                 vmem((ITERS + 1, *wide), F32),
                 vmem((ITERS, n_row * n_lo, 1, lanes), F32),
-                dma((15,)),
-                dma((n_row,)),
-                dma((n_row,)),
-                dma((n_row,)),
-                dma((n_row,)),
-                dma((ITERS, n_row)),
-                dma((ITERS, n_row)),
-                dma((ITERS + 1, n_lo)),
-                dma((ITERS + 1, n_lo)),
-                dma((ITERS + 1, n_hi)),
-                dma((ITERS + 1, n_hi)),
-                dma((ITERS + 1, n_lo)),
-                dma((ITERS + 1, n_lo)),
-                dma((ITERS, n_row * n_lo)),
-                dma((ITERS, n_row * n_lo)),
+                dma((6,)),
+                dma(()),
+                dma(()),
+                dma(()),
+                dma(()),
+                dma((ITERS,)),
+                dma((ITERS,)),
+                *[dma((ITERS + 1,))] * 6,
+                dma((ITERS,)),
+                dma((ITERS,)),
             ],
             compiler_params=pltpu.CompilerParams(collective_id=0, has_side_effects=True),
             name="admm",
@@ -402,13 +379,16 @@
         )
         x_new, z_new, y_new = pl.pallas_call(
             unpack,
+            in_specs=[pl.BlockSpec(memory_space=vmem)],
+            out_specs=(pl.BlockSpec(memory_space=pl.ANY),) * 3,
+            scratch_shapes=[vmem((width, xb), F32), dma((3,))],
             out_shape=(
                 jax.ShapeDtypeStruct((width, xb), F32),
                 jax.ShapeDtypeStruct((zb, lanes), F32),
                 jax.ShapeDtypeStruct((zb, lanes), F32),
             ),
             name="unpack",
-        )(packed)
+        )(pltpu.with_memory_space_constraint(packed, vmem))
         return x_new.T, z_new, y_new
 
     placed = (

time: 82.3 us -> 76.5 us (0.930)
  Pallas kernels: 79.6 us -> 73.8 us
    pallas_call x2, Pallas kernels: 79.6 us -> 73.8 us  [the longest x1 73.1 us: shards(): pl.pallas_call(functools.partial(kernel, dims), out_shape=vmem((2 * zb +...]
where the time goes in v3:
time: 76.5 us; the launch traced here: 76.4 us
  Pallas kernels  73.8 us (96%)
  between operations  2.58 us (3%)
    pallas_call x1, Pallas kernels, shards(): pl.pallas_call(functools.partial(kernel, dims), out_shape=vmem((2 * zb +...  73.1 us

profile of v3, /device:TPU:1, one launch (start us, length us, event | category | flops | bytes accessed | tf_op | source)
XLA Modules:
  0.0 76.4 jit_solution(4357893303275642902)
XLA Ops:
  2.6 73.1 %admm.1.packed = f32[336,128]{1,0:T(8,128)S(1)} custom-call(f32[1]{0:T(128)S(6)} %copy.16.rho_ref, f32[1]{0:T(128)S(6)} %copy.17.sigma_ref, f32[1]{0:T(128)S(6)} %copy.18.relax_ref, s32[1,64]{1,0:T(1,128)} %bitcast.11, s32[1,64]{1,0:T(1,128)} %bitcast.12, f32[16,24]{1,0:T(8,128)} %bitcast.8, f32[16,24]{1,0:T(8,128)} %bitcast.9, f32[16,24]{1,0:T(8,128)} %bitcast.10, ...), custom_call_target="tpu_custom_call" | custom-call | tf_op jit(solution)/shard_map/admm/pallas_call | solution.py:335
  75.7 0.7 unpack.1

commit v4 on v3

--- a/solution.py
+++ b/solution.py
@@ -8,6 +8,7 @@
 from jax.sharding import PartitionSpec as P
 
 ITERS = 2
+ON_MXU = 48
 MESH = pl.DeviceIdType.MESH
 F32 = jnp.float32
 BF16 = jnp.bfloat16
@@ -50,6 +51,8 @@
     plain_buf,
     tiles,
     turned,
+    forward_weights,
+    backward_weights,
     acc,
     picked,
     vector_buf,
@@ -108,9 +111,11 @@
         other = lax.rem(lo + step, n_lo)
         return other, (row, hi * n_lo + other)
 
+    far = sorted(((a, b) for a in range(n_row) for b in range(n_lo)), key=lambda s: abs(s[0] - n_row / 2) + abs(s[1] - n_lo / 2))
+
     def plane_peer(step):
-        other_row = lax.rem(row + step // n_lo, n_row)
-        other_lo = lax.rem(lo + step % n_lo, n_lo)
+        other_row = lax.rem(row + far[step - 1][0], n_row)
+        other_lo = lax.rem(lo + far[step - 1][1], n_lo)
         return other_row * n_lo + other_lo, (other_row, hi * n_lo + other_lo)
 
     n_plane = n_row * n_lo
@@ -155,6 +160,13 @@
         copies.wait_recv()
         copies.wait_send()
 
+    def weigh(weights, tile_of):
+        for k in range(ON_MXU):
+            heads, rest = pieces(tile_of(k), 2)
+            side = slice(lanes * (k % 2), lanes * (k % 2 + 1))
+            weights[k // 2, 0:lanes, side] = heads
+            weights[k // 2, lanes : 2 * lanes, side] = rest
+
     empty = jnp.zeros((width, lanes - xb), F32)
     loaded(0, small_buf)
     loaded(1, index_buf)
@@ -180,21 +192,34 @@
 
     loaded(4, plain_buf)
     loaded(5, tiles)
-    for k in range(count):
-        turned[k] = tiles[k].T
+    weigh(forward_weights, lambda k: tiles[k].T)
+    for k in range(ON_MXU, count):
+        turned[k - ON_MXU] = tiles[k].T
     for index, ref in enumerate((zs, ys, low, high)):
-        ref[...] = jnp.zeros_like(ref)
         for k in range(n_lo):
-            ref[k, 0:piece, :] = plain_buf[index, k * piece : (k + 1) * piece, :]
+            ref[k] = plain_buf[index, k * piece : (k + 1) * piece, :]
 
     rho = rho_ref[0]
     sigma = sigma_ref[0]
     relax = relax_ref[0]
 
-    def products(which):
-        columns = picked[...].T
-        for k in range(count):
-            terms = which[k] * columns[:, k : k + 1]
+    def products(weights, plain):
+        vectors = picked[...]
+        none = jnp.zeros((8, lanes), F32)
+        for first in range(0, ON_MXU, 8):
+            vector = vectors[first : first + 8]
+            heads = vector.astype(BF16).astype(F32)
+            top = jnp.concatenate([heads, heads], axis=1)
+            bottom = jnp.concatenate([vector - heads, none], axis=1)
+            left = jnp.concatenate([top, bottom], axis=0).astype(BF16)
+            for k in range(0, 8, 2):
+                both = jnp.dot(left, weights[(first + k) // 2], preferred_element_type=F32)
+                both = both[:8] + both[8:]
+                acc[first + k : first + k + 1, :] = both[k : k + 1, :lanes]
+                acc[first + k + 1 : first + k + 2, :] = both[k + 1 : k + 2, lanes:]
+        columns = vectors.T
+        for k in range(ON_MXU, count):
+            terms = plain(k) * columns[:, k : k + 1]
             acc[k : k + 1, :] = jnp.sum(terms, axis=0, keepdims=True)
         return acc[...]
 
@@ -202,28 +227,29 @@
         vector_buf[0:xb, :] = vector
         for k in range(count):
             picked[k : k + 1, :] = vector_buf[pl.ds(cols_ref[0, k], 1), :]
-        part = select(row_sum[...], products(turned))
+        part = select(row_sum[...], products(forward_weights, lambda k: turned[k - ON_MXU]))
         part_buf[turn] = part.reshape(n_lo, pad, lanes)
         for k, value in enumerate(scalars):
             for slot in range(n_lo):
                 part_buf[turn, slot, piece + k : piece + k + 1, :] = value
         rs_buf[turn, lo] = part_buf[turn, lo]
-        parts = part_buf.at[turn]
-        scatter = (n_lo, lo_peer, lambda other: parts.at[other], rs_buf.at[turn], lo, rs_send.at[turn], rs_recv.at[turn])
+        used = pl.ds(0, piece + len(scalars))
+        parts = part_buf.at[turn, :, used]
+        landed = rs_buf.at[turn, :, used]
+        scatter = (n_lo, lo_peer, lambda other: parts.at[other], landed, lo, rs_send.at[turn], rs_recv.at[turn])
         exchange(*scatter)
         yield
         arrive(*scatter)
-        ar_buf[turn, hi] = sum(rs_buf[turn, k] for k in range(n_lo))
-        sums = ar_buf.at[turn]
+        sums = ar_buf.at[turn, :, used]
+        sums[hi] = sum(landed[k] for k in range(n_lo))
         reduce = (n_hi, hi_peer, lambda other: sums.at[hi], sums, hi, ar_send.at[turn], ar_recv.at[turn])
         exchange(*reduce)
         yield
         arrive(*reduce)
-        whole = sum(ar_buf[turn, k] for k in range(n_hi))
-        inside = lax.broadcasted_iota(jnp.int32, whole.shape, 0) < piece
-        kept = jnp.where(inside, whole, 0.0)
-        ag_buf[turn, lo] = kept
-        wholes = ag_buf.at[turn]
+        whole = sum(sums[k] for k in range(n_hi))
+        kept = whole[:piece]
+        wholes = ag_buf.at[turn, :, pl.ds(0, piece)]
+        wholes[lo] = kept
         gather = (n_lo, lo_peer, lambda other: wholes.at[lo], wholes, lo, ag_send.at[turn], ag_recv.at[turn])
         exchange(*gather)
         if scalars:
@@ -241,21 +267,23 @@
     xs[...] = jnp.concatenate([start_buf[k] for k in range(n_row)], axis=0).T[:xb]
     stages = forward(xs[...], [], 0)
     next(stages)
+    weigh(backward_weights, lambda k: tiles[k])
     arrive(*cost)
     diag[...] = jnp.concatenate([cost_buf[k, 0] for k in range(n_row)], axis=0).T[:xb]
     lin[...] = jnp.concatenate([cost_buf[k, 1] for k in range(n_row)], axis=0).T[:xb]
     for _ in stages:
         pass
-    image[...] = ag_buf[0]
+    for k in range(n_lo):
+        image[k] = ag_buf[0, k, 0:piece, :]
 
     def iteration(turn, carry):
         for k in range(n_lo):
-            vector_buf[k * pad : (k + 1) * pad, :] = rho * zs[k] - ys[k] - rho * image[k]
+            vector_buf[k * pad : k * pad + piece, :] = rho * zs[k] - ys[k] - rho * image[k]
         for k in range(count):
             index = rows_ref[0, k]
             index = index + (pad - piece) * (index // piece)
             picked[k : k + 1, :] = vector_buf[pl.ds(index, 1), :]
-        back_buf[turn, row] = select(col_sum[...], products(tiles))
+        back_buf[turn, row] = select(col_sum[...], products(backward_weights, lambda k: tiles[k]))
         backs = back_buf.at[turn]
         back = (n_row, row_peer, lambda other: backs.at[row], backs, row, back_send.at[turn], back_recv.at[turn])
         exchange(*back)
@@ -279,7 +307,7 @@
         xs[...] = relax * (x_now + step * residual) + (1.0 - relax) * x_now
         for k in range(n_lo):
             old = image[k]
-            moved = old + step * ag_buf[turn + 1, k]
+            moved = old + step * ag_buf[turn + 1, k, 0:piece, :]
             image[k] = relax * moved + (1.0 - relax) * old
             mixed = relax * moved + (1.0 - relax) * zs[k]
             y_now = ys[k]
@@ -291,8 +319,8 @@
     lax.fori_loop(0, ITERS, iteration, 0)
 
     for k in range(n_lo):
-        out[k * piece : (k + 1) * piece, :] = zs[k, 0:piece, :]
-        out[zb + k * piece : zb + (k + 1) * piece, :] = ys[k, 0:piece, :]
+        out[k * piece : (k + 1) * piece, :] = zs[k]
+        out[zb + k * piece : zb + (k + 1) * piece, :] = ys[k]
     mine = pltpu.roll(xs[...], lax.rem(lanes - width * row, lanes), axis=1)
     mine = jnp.concatenate([mine, jnp.zeros((lanes - xb, lanes), F32)], axis=0)
     out[2 * zb : 2 * zb + width, :] = mine.T[:width]
@@ -344,13 +372,15 @@
                 vmem((3, width, xb), F32),
                 vmem((4, zb, lanes), F32),
                 vmem((count, order, order), F32),
-                vmem((count, order, order), F32),
+                vmem((count - ON_MXU, order, order), F32),
+                vmem((ON_MXU // 2, 2 * order, 2 * order), BF16),
+                vmem((ON_MXU // 2, 2 * order, 2 * order), BF16),
                 vmem((count, lanes), F32),
                 vmem((count, lanes), F32),
                 vmem((n_lo * pad, lanes), F32),
                 vmem((n_lo * pad, count), BF16),
                 vmem((xb, count), BF16),
-                *[vmem(wide, F32)] * 5,
+                *[vmem((n_lo, piece, lanes), F32)] * 5,
                 *[vmem((xb, lanes), F32)] * 3,
                 vmem((n_row, width, lanes), F32),
                 vmem((n_row, 2, width, lanes), F32),

time: 76.5 us -> 71.4 us (0.933)
  Pallas kernels: 73.8 us -> 68.7 us
    pallas_call x1, Pallas kernels: 73.1 us -> 68 us  [shards(): pl.pallas_call(functools.partial(kernel, dims), out_shape=vmem((2 * zb +...]
where the time goes in v4:
time: 71.4 us; the launch traced here: 71.3 us
  Pallas kernels  68.7 us (96%)
  between operations  2.58 us (4%)
    pallas_call x1, Pallas kernels, shards(): pl.pallas_call(functools.partial(kernel, dims), out_shape=vmem((2 * zb +...  68 us

profile of v4, /device:TPU:1, one launch (start us, length us, event | category | flops | bytes accessed | tf_op | source)
XLA Modules:
  0.0 71.3 jit_solution(13795476171595827623)
XLA Ops:
  2.6 68.0 %admm.1.packed = f32[336,128]{1,0:T(8,128)S(1)} custom-call(f32[1]{0:T(128)S(6)} %copy.16.rho_ref, f32[1]{0:T(128)S(6)} %copy.17.sigma_ref, f32[1]{0:T(128)S(6)} %copy.18.relax_ref, s32[1,64]{1,0:T(1,128)} %bitcast.11, s32[1,64]{1,0:T(1,128)} %bitcast.12, f32[16,24]{1,0:T(8,128)} %bitcast.8, f32[16,24]{1,0:T(8,128)} %bitcast.9, f32[16,24]{1,0:T(8,128)} %bitcast.10, ...), custom_call_target="tpu_custom_call" | custom-call | tf_op jit(solution)/shard_map/admm/pallas_call | solution.py:363
  70.6 0.7 unpack.1

commit v5 on v4

--- a/solution.py
+++ b/solution.py
@@ -46,6 +46,7 @@
     out,
     rows_ref,
     cols_ref,
+    places_ref,
     index_buf,
     small_buf,
     plain_buf,
@@ -99,38 +100,49 @@
     hi = lax.div(col, n_lo)
     lo = lax.rem(col, n_lo)
 
+    def away(size):
+        return sorted(range(size), key=lambda k: -min(k, size - k))
+
+    pairs = [(a, b) for a in away(n_row // 2) for b in (1, 0)]
+
+    def moved(place, pair):
+        outer, inner = lax.div(place, 2), lax.rem(place, 2)
+        return lax.rem(outer + pair[0], n_row // 2) * 2 + (1 - inner if pair[1] else inner)
+
     def row_peer(step):
-        other = lax.rem(row + step, n_row)
+        other = moved(row, pairs[step - 1])
         return other, (other, col)
 
     def hi_peer(step):
-        other = lax.rem(hi + step, n_hi)
+        other = lax.rem(hi + away(n_hi)[step - 1], n_hi)
         return other, (row, other * n_lo + lo)
 
     def lo_peer(step):
-        other = lax.rem(lo + step, n_lo)
+        other = moved(lo, pairs[step - 1])
         return other, (row, hi * n_lo + other)
 
-    far = sorted(((a, b) for a in range(n_row) for b in range(n_lo)), key=lambda s: abs(s[0] - n_row / 2) + abs(s[1] - n_lo / 2))
+    def hops(pair):
+        return min(pair[0], n_row // 2 - pair[0]) + 0.5 * pair[1]
+
+    planes = sorted(((a, b) for a in pairs for b in pairs), key=lambda ab: -hops(ab[0]) - hops(ab[1]))
 
     def plane_peer(step):
-        other_row = lax.rem(row + far[step - 1][0], n_row)
-        other_lo = lax.rem(lo + far[step - 1][1], n_lo)
+        other_row, other_lo = moved(row, planes[step - 1][0]), moved(lo, planes[step - 1][1])
         return other_row * n_lo + other_lo, (other_row, hi * n_lo + other_lo)
 
     n_plane = n_row * n_lo
     plane = row * n_lo + lo
-
-    barrier = pltpu.get_barrier_semaphore()
-    for size, peer in ((n_plane, plane_peer), (n_hi, hi_peer)):
-        for step in range(1, size):
-            pl.semaphore_signal(barrier, inc=1, device_id=peer(step)[1], device_id_type=MESH)
 
     smalls = [(x0_hbm, small_buf.at[0], 0), (diag0_hbm, small_buf.at[1], 0), (lin0_hbm, small_buf.at[2], 0)]
     indices = [(rows_hbm, index_buf.at[0], 1), (cols_hbm, index_buf.at[1], 1), (rows_hbm, rows_ref, 2), (cols_hbm, cols_ref, 3)]
     plains = [(ref, plain_buf.at[k], 4) for k, ref in enumerate((z0_hbm, y0_hbm, low0_hbm, high0_hbm))]
     for source, target, k in [*smalls, *indices, *plains, (tiles_hbm, tiles, 5)]:
         pltpu.make_async_copy(source, target, load_sem.at[k]).start()
+
+    barrier = pltpu.get_barrier_semaphore()
+    for size, peer in ((n_row, row_peer), (n_lo, lo_peer), (n_hi, hi_peer)):
+        for step in range(1, size):
+            pl.semaphore_signal(barrier, inc=1, device_id=peer(step)[1], device_id_type=MESH)
 
     def loaded(k, target):
         pltpu.make_async_copy(target, target, load_sem.at[k]).wait()
@@ -167,13 +179,20 @@
             weights[k // 2, 0:lanes, side] = heads
             weights[k // 2, lanes : 2 * lanes, side] = rest
 
+    loaded(0, small_buf)
     empty = jnp.zeros((width, lanes - xb), F32)
-    loaded(0, small_buf)
-    loaded(1, index_buf)
     start_buf[row] = jnp.concatenate([small_buf[0], empty], axis=1)
     for k in range(2):
         cost_buf[row, k] = jnp.concatenate([small_buf[k + 1], empty], axis=1)
 
+    pl.semaphore_wait(barrier, n_row + n_lo + n_hi - 3)
+
+    start = (n_row, row_peer, lambda other: start_buf.at[row], start_buf, row, start_send, start_recv)
+    exchange(*start)
+    cost = (n_row, row_peer, lambda other: cost_buf.at[row], cost_buf, row, cost_send, cost_recv)
+    exchange(*cost)
+
+    loaded(1, index_buf)
     rows = index_buf[0]
     padded = rows
     for k in range(1, n_lo):
@@ -182,13 +201,9 @@
     col_sum[...] = (lax.broadcasted_iota(jnp.int32, (xb, count), 0) == index_buf[1]).astype(BF16)
     loaded(2, rows_ref)
     loaded(3, cols_ref)
-
-    pl.semaphore_wait(barrier, n_plane - 1 + n_hi - 1)
-
-    start = (n_row, row_peer, lambda other: start_buf.at[row], start_buf, row, start_send, start_recv)
-    exchange(*start)
-    cost = (n_row, row_peer, lambda other: cost_buf.at[row], cost_buf, row, cost_send, cost_recv)
-    exchange(*cost)
+    for k in range(count):
+        index = rows_ref[0, k]
+        places_ref[k] = index + (pad - piece) * (index // piece)
 
     loaded(4, plain_buf)
     loaded(5, tiles)
@@ -280,9 +295,7 @@
         for k in range(n_lo):
             vector_buf[k * pad : k * pad + piece, :] = rho * zs[k] - ys[k] - rho * image[k]
         for k in range(count):
-            index = rows_ref[0, k]
-            index = index + (pad - piece) * (index // piece)
-            picked[k : k + 1, :] = vector_buf[pl.ds(index, 1), :]
+            picked[k : k + 1, :] = vector_buf[pl.ds(places_ref[k], 1), :]
         back_buf[turn, row] = select(col_sum[...], products(backward_weights, lambda k: tiles[k]))
         backs = back_buf.at[turn]
         back = (n_row, row_peer, lambda other: backs.at[row], backs, row, back_send.at[turn], back_recv.at[turn])
@@ -368,6 +381,7 @@
             scratch_shapes=[
                 smem((1, count), jnp.int32),
                 smem((1, count), jnp.int32),
+                smem((count,), jnp.int32),
                 vmem((2, 1, count), jnp.int32),
                 vmem((3, width, xb), F32),
                 vmem((4, zb, lanes), F32),

time: 71.4 us -> 68.5 us (0.959)
  Pallas kernels: 68.7 us -> 65.8 us
    pallas_call x1, Pallas kernels: 68 us -> 65.1 us  [shards(): pl.pallas_call(functools.partial(kernel, dims), out_shape=vmem((2 * zb +...]
where the time goes in v5:
time: 68.5 us; the launch traced here: 68.4 us
  Pallas kernels  65.8 us (96%)
  between operations  2.58 us (4%)
    pallas_call x1, Pallas kernels, shards(): pl.pallas_call(functools.partial(kernel, dims), out_shape=vmem((2 * zb +...  65.1 us

profile of v5, /device:TPU:1, one launch (start us, length us, event | category | flops | bytes accessed | tf_op | source)
XLA Modules:
  0.0 68.4 jit_solution(16409403655573525659)
XLA Ops:
  2.6 65.1 %admm.1.packed = f32[336,128]{1,0:T(8,128)S(1)} custom-call(f32[1]{0:T(128)S(6)} %copy.16.rho_ref, f32[1]{0:T(128)S(6)} %copy.17.sigma_ref, f32[1]{0:T(128)S(6)} %copy.18.relax_ref, s32[1,64]{1,0:T(1,128)} %bitcast.11, s32[1,64]{1,0:T(1,128)} %bitcast.12, f32[16,24]{1,0:T(8,128)} %bitcast.8, f32[16,24]{1,0:T(8,128)} %bitcast.9, f32[16,24]{1,0:T(8,128)} %bitcast.10, ...), custom_call_target="tpu_custom_call" | custom-call | tf_op jit(solution)/shard_map/admm/pallas_call | solution.py:376
  67.7 0.7 %unpack.1 = (f32[16,24]{1,0:T(8,128)}, f32[160,128]{1,0:T(8,128)}, f32[160,128]{1,0:T(8,128)}) custom-call(f32[336,128]{1,0:T(8,128)S(1)} %admm.1.packed), custom_call_target="tpu_custom_call" | custom-call | tf_op jit(solution)/shard_map/unpack/pallas_call | solution.py:424
